TPU v7x, 32 devices: a whole 2x2x4 slice. The times are simulated.
32 devices in a mesh: rows: 16 (over z, x, core), cols: 2 (over y).
Axes of the slice: x: 2, y: 2, z: 4, core: 2. Of those that a mesh axis runs over, the one named last changes fastest.
Arguments:
- columns: float32 [512, 16384], P('cols', 'rows'), may hold values from -200 to 200
Outputs:
- orthonormal: float32 [256, 16384], P('cols', 'rows')
- triangle: float32 [256, 512], P('cols')
- trailing: float32 [256, 16384], P('cols', 'rows')
All inputs are finite; a program needn't handle non-finite values.
Results may differ from a plain program's by a relative error of at most 0.00008.
Values sent between devices are 32-bit elements; how exact they have to be, the bound alone decides.
A program may use at most 64 MiB of HBM per device.

v0:
```python
import functools
import math

import jax
import jax.numpy as jnp
from jax import lax
from jax.experimental import pallas as pl
from jax.experimental.pallas import tpu as pltpu
from jax.sharding import PartitionSpec as P

PANEL = 128
STRIP = 16
VMEM_BYTES = 20 * 2**20
MESH = pl.DeviceIdType.MESH

precise = lax.Precision.HIGHEST


def product(left, right):
    return jnp.dot(left, right, precision=precise, preferred_element_type=jnp.float32)


def contract(left, right, dims):
    return lax.dot_general(
        left, right, (dims, ((), ())), precision=precise, preferred_element_type=jnp.float32
    )


def across_rows(left, right):
    return contract(left, right, ((1,), (1,)))


def pieces(value):
    first = value.astype(jnp.bfloat16)
    rest = value - first.astype(jnp.float32)
    second = rest.astype(jnp.bfloat16)
    third = (rest - second.astype(jnp.float32)).astype(jnp.bfloat16)
    return first, second, third


def strip_update(left, right):
    a, b, c = pieces(left)
    d, e, f = pieces(right)
    lhs = jnp.concatenate([a, a, b, a, c, b], axis=0)
    rhs = jnp.concatenate([d, e, d, f, d, e], axis=0)
    return lax.dot_general(
        lhs, rhs, (((0,), (0,)), ((), ())), preferred_element_type=jnp.float32
    )


def eliminate(ref, hooks):
    size = ref.shape[0]
    lanes = size
    parts = ref.shape[1] // lanes
    below = lax.broadcasted_iota(jnp.int32, (STRIP, lanes), 0)
    for s in range(size // STRIP):
        at = s * STRIP
        rows = [ref[at:at + STRIP, q * lanes:(q + 1) * lanes] for q in range(parts)]
        cols = [
            jnp.broadcast_to(rows[0][:, at + j:at + j + 1], (STRIP, lanes))
            for j in range(STRIP)
        ]
        for i in range(STRIP):
            pivot = cols[i][i:i + 1]
            inv = lax.rsqrt(pivot)
            inv = inv * (1.5 - 0.5 * pivot * inv * inv)
            col = cols[i] * inv
            coef = jnp.where(below > i, col, 0.0)
            for j in range(i + 1, STRIP):
                cols[j] = cols[j] - coef * col[j:j + 1]
            for q in range(parts):
                row = rows[q][i:i + 1] * inv
                rows[q] = jnp.where(below == i, row, rows[q] - coef * row)
        for q in range(parts):
            ref[at:at + STRIP, q * lanes:(q + 1) * lanes] = rows[q]
        after = at + STRIP
        if after < size:
            update = strip_update(rows[0], jnp.concatenate(rows, axis=1))
            ref[after:, :] = ref[after:, :] - update[after:, :]
        if s in hooks:
            hooks[s]()


def kernel(row_count, scaling, x_ref, qs, tri_ref, tail_ref, coup_ref,
           xs, ys, part, gram, pair_in, ring_in, first, second,
           xy, xy_pair, xy_ring, xy_own, xy_other, coupled, send, recv_x, recv_pair,
           recv_ring, recv_all, recv_half, recv_y):
    r = lax.axis_index("rows")
    c = lax.axis_index("cols")
    other = 1 - c
    parity = lax.rem(r, 2)
    h = r // 2
    mates = row_count // 2
    partner = (r + 1 - 2 * parity, c)
    across = (r, other)
    size = PANEL

    def mate(k):
        idx = lax.rem(h + k, mates)
        return idx, (idx * 2 + parity, c)

    barrier = pltpu.get_barrier_semaphore()
    for target in [partner, across] + [mate(k)[1] for k in range(1, mates)]:
        pl.semaphore_signal(barrier, inc=1, device_id=target, device_id_type=MESH)
    pl.semaphore_wait(barrier, mates + 1)

    def push(src, dst, send_sem, recv_sem, target):
        return pltpu.make_async_remote_copy(
            src_ref=src, dst_ref=dst, send_sem=send_sem, recv_sem=recv_sem,
            device_id=target, device_id_type=MESH)

    width = x_ref.shape[1]
    eighth = width // 8
    early = pl.ds(0, 4 * eighth)
    late = pl.ds(4 * eighth, 4 * eighth)
    spans = ((4, 3), (7, 1), (0, 3), (3, 1))

    def x_copy(q):
        span = pl.ds(spans[q][0] * eighth, spans[q][1] * eighth)
        return push(x_ref.at[:, span], xs.at[:, span], send.at[q], recv_x.at[q], across)

    def y_copy(q):
        view = (pl.ds(0, 2 * size), early) if q == 0 else (pl.ds(0, size), late)
        return push(x_ref.at[view], ys.at[view], send.at[q], recv_x.at[q], across)

    @pl.when(c == 0)
    def _():
        x_copy(0).start()

    @pl.when(c == 1)
    def _():
        y_copy(0).start()
        y_copy(1).start()
        ys[...] = x_ref[...]

    def spread(base, full, pair_buf, ring_buf, tag):
        half = full.shape[0] // 2
        chunk = half // mates
        mine = pl.ds(parity * half, half)
        his = pl.ds((1 - parity) * half, half)
        own = pl.ds(pl.multiple_of(parity * half + h * chunk, 8), chunk)

        def pair_copy():
            return push(full.at[his], pair_buf, send.at[base],
                        recv_pair.at[tag], partner)

        def ring_copy(k):
            idx, target = mate(k)
            return push(
                full.at[pl.ds(pl.multiple_of(parity * half + idx * chunk, 8), chunk)],
                ring_buf.at[k], send.at[base + k], recv_ring.at[tag * mates + k], target)

        def gather_copy(dst, k):
            return push(dst.at[own], dst.at[own], send.at[base + mates + k],
                        recv_all.at[tag * mates + k], mate(k)[1])

        def gather_wait(dst, k):
            idx = lax.rem(h + mates - k, mates)
            there = pl.ds(pl.multiple_of(parity * half + idx * chunk, 8), chunk)
            push(dst.at[there], dst.at[there], send.at[base + mates + k],
                 recv_all.at[tag * mates + k], mate(k)[1]).wait_recv()

        def half_copy(dst):
            return push(dst.at[mine], dst.at[mine], send.at[base + 2 * mates],
                        recv_half.at[tag], partner)

        def half_wait(dst):
            push(dst.at[his], dst.at[his], send.at[base + 2 * mates],
                 recv_half.at[tag], partner).wait_recv()

        def start_pair():
            pair_copy().start()

        def start_ring():
            pair_copy().wait_recv()
            full[mine] = full[mine] + pair_buf[...]
            for k in range(1, mates):
                ring_copy(k).start()

        def finish_ring():
            for k in range(1, mates):
                ring_copy(k).wait_recv()
            total = full[own]
            for k in range(1, mates):
                total = total + ring_buf[k]
            return total

        def drain_scatter():
            pair_copy().wait_send()
            for k in range(1, mates):
                ring_copy(k).wait_send()

        def start_gather(dst):
            for k in range(1, mates):
                gather_copy(dst, k).start()

        def start_half(dst):
            for k in range(1, mates):
                gather_wait(dst, k)
            half_copy(dst).start()

        def finish(dst):
            half_wait(dst)

        def drain_gather(dst):
            for k in range(1, mates):
                gather_copy(dst, k).wait_send()
            half_copy(dst).wait_send()

        return (start_pair, start_ring, finish_ring, drain_scatter, start_gather,
                start_half, finish, drain_gather, own)

    base_g = 4
    (g_pair, g_ring, g_sum, g_drain, g_gather, g_half, g_finish, g_drain_all,
     g_own) = spread(base_g, part, pair_in, ring_in, 0)
    base_y = base_g + 2 * mates + 2
    y_send = send.at[base_g + 2 * mates + 1]

    def chunk_copy():
        return push(gram.at[g_own], gram.at[g_own], y_send, recv_y.at[0], across)

    (y_pair, y_ring, y_sum, y_drain, y_gather, y_half, y_finish, y_drain_all,
     y_own) = spread(base_y, xy, xy_pair, xy_ring, 1)

    @pl.when(c == 0)
    def _():
        strip = across_rows(x_ref[:size], x_ref[...])
        part[:size] = strip[:, :size]
        part[size:2 * size] = strip[:, size:]
        part[2 * size:] = across_rows(x_ref[size:, :], x_ref[size:, :])
        g_pair()
        xs[...] = x_ref[...]
        g_ring()
        gram[g_own] = g_sum()
        chunk_copy().start()
        x_copy(1).start()
        x_copy(2).start()

    @pl.when(c == 1)
    def _():
        chunk_copy().wait_recv()

    g_gather(gram)
    g_half(gram)

    @pl.when(c == 0)
    def _():
        y_copy(0).wait_recv()
        xy[...] = across_rows(xs[:, early], ys[:, early])

    @pl.when(c == 1)
    def _():
        x_copy(0).wait_recv()
        x_copy(1).wait_recv()
        xy[...] = across_rows(xs[:, late], ys[:, late])

    y_pair()
    g_finish(gram)

    eye = (lax.broadcasted_iota(jnp.int32, (size, size), 0)
           == lax.broadcasted_iota(jnp.int32, (size, size), 1)).astype(jnp.float32)
    first[:, :size] = gram[:size]
    first[:, size:2 * size] = gram[size:2 * size]
    first[:, 2 * size:] = eye

    def swap_copy():
        return push(xy_own, xy_other, send.at[base_y + 2 * mates + 1], recv_y.at[1], across)

    def hook_sum():
        xy_own[...] = y_sum()
        swap_copy().start()

        @pl.when(c == 0)
        def _():
            x_copy(3).start()

    def hook_gather():
        swap_copy().wait_recv()
        coupled[y_own] = xy_own[...] + xy_other[...]
        y_gather(coupled)

    eliminate(first, {0: y_ring, 6: hook_sum})

    upper = first[:, size:2 * size]
    cross = contract(upper, first[:, size:], ((0,), (0,)))
    second[:, :size] = gram[2 * size:] - cross[:, :size]
    second[:, size:2 * size] = -cross[:, size:]
    second[:, 2 * size:] = eye
    eliminate(second, {0: hook_gather, 7: lambda: y_half(coupled)})

    @pl.when(c == 1)
    def _():
        x_copy(2).wait_recv()
        x_copy(3).wait_recv()

    inv00 = first[:, 2 * size:]
    inv1 = second[:, size:]
    qs[:size] = product(inv00, xs[:size])
    qs[size:] = product(inv1, xs[...])
    own_rows = pl.ds(pl.multiple_of(c * size, size), size)

    @pl.when(c == 0)
    def _():
        y_copy(1).wait_recv()

    tail_ref[...] = ys[own_rows]
    y_finish(coupled)
    mine = coupled[:, pl.ds(pl.multiple_of(c * size, size), size)]
    coup_ref[:size] = product(inv00, mine[:size])
    coup_ref[size:] = product(inv1, mine)

    keep = (lax.broadcasted_iota(jnp.int32, (size, size), 0)
            <= lax.broadcasted_iota(jnp.int32, (size, size), 1))

    @pl.when(c == 0)
    def _():
        tri_ref[:, :size] = jnp.where(keep, first[:, :size], 0.0) / scaling
        tri_ref[:, size:2 * size] = first[:, size:2 * size] / scaling
        tri_ref[:, 2 * size:] = product(inv00, coupled[:size]) / scaling
        for q in range(4):
            x_copy(q).wait_send()
        g_drain()
        chunk_copy().wait_send()

    @pl.when(c == 1)
    def _():
        tri_ref[:, :size] = jnp.zeros((size, size), jnp.float32)
        tri_ref[:, size:2 * size] = jnp.where(keep, second[:, :size], 0.0) / scaling
        tri_ref[:, 2 * size:] = product(inv1, coupled[...]) / scaling
        for q in range(2):
            y_copy(q).wait_send()

    g_drain_all(gram)
    y_drain()
    y_drain_all(coupled)
    swap_copy().wait_send()


def finish_kernel(scaling, q_ref, tri_in, tail_in, coup_ref, ortho_ref, tri_ref, trail_ref):
    size = coup_ref.shape[1]
    own_rows = pl.ds(pl.multiple_of(lax.axis_index("cols") * size, size), size)
    ortho_ref[...] = q_ref[own_rows] * scaling
    trail_ref[...] = tail_in[...] - contract(coup_ref[...], q_ref[...], ((0,), (0,)))

    @pl.when(pl.program_id(0) == 0)
    def _():
        tri_ref[...] = tri_in[...]


def fused(columns):
    row_count = lax.axis_size("rows")
    width = columns.shape[1]
    scaling = math.sqrt(width * row_count)
    size = PANEL
    mates = row_count // 2
    f32 = jnp.float32
    vmem = pl.BlockSpec(memory_space=pltpu.VMEM)
    ortho = jax.ShapeDtypeStruct((size, width), f32)
    triangle = jax.ShapeDtypeStruct((size, 4 * size), f32)
    trailing = ortho
    middle = pl.pallas_call(
        functools.partial(kernel, row_count, scaling),
        out_shape=(
            jax.ShapeDtypeStruct((2 * size, width), f32),
            triangle,
            trailing,
            jax.ShapeDtypeStruct((2 * size, size), f32),
        ),
        in_specs=[vmem],
        out_specs=(vmem, vmem, vmem, vmem),
        scratch_shapes=[
            pltpu.VMEM((2 * size, width), f32),
            pltpu.VMEM((2 * size, width), f32),
            pltpu.VMEM((3 * size, size), f32),
            pltpu.VMEM((3 * size, size), f32),
            pltpu.VMEM((3 * size // 2, size), f32),
            pltpu.VMEM((mates, 3 * size // row_count, size), f32),
            pltpu.VMEM((size, 3 * size), f32),
            pltpu.VMEM((size, 3 * size), f32),
            pltpu.VMEM((2 * size, 2 * size), f32),
            pltpu.VMEM((size, 2 * size), f32),
            pltpu.VMEM((mates, 2 * size // row_count, 2 * size), f32),
            pltpu.VMEM((2 * size // row_count, 2 * size), f32),
            pltpu.VMEM((2 * size // row_count, 2 * size), f32),
            pltpu.VMEM((2 * size, 2 * size), f32),
            pltpu.SemaphoreType.DMA((4 + 2 * (2 * mates + 2),)),
            pltpu.SemaphoreType.DMA((4,)),
            pltpu.SemaphoreType.DMA((2,)),
            pltpu.SemaphoreType.DMA((2 * mates,)),
            pltpu.SemaphoreType.DMA((2 * mates,)),
            pltpu.SemaphoreType.DMA((2,)),
            pltpu.SemaphoreType.DMA((2,)),
        ],
        compiler_params=pltpu.CompilerParams(
            collective_id=0, has_side_effects=True, vmem_limit_bytes=VMEM_BYTES),
    )(columns)
    steps = 2
    span = width // steps

    def along(rows):
        return pl.BlockSpec((rows, span), lambda i: (0, i))

    def whole(shape):
        return pl.BlockSpec(shape, lambda i: (0, 0))

    return pl.pallas_call(
        functools.partial(finish_kernel, scaling),
        grid=(steps,),
        out_shape=(ortho, triangle, trailing),
        in_specs=[along(2 * size), whole(triangle.shape), along(size), whole((2 * size, size))],
        out_specs=(along(size), whole(triangle.shape), along(size)),
        compiler_params=pltpu.CompilerParams(vmem_limit_bytes=VMEM_BYTES),
    )(*middle)


def inverse_lower(lower):
    identity = jnp.eye(lower.shape[0], dtype=lower.dtype)
    return lax.linalg.triangular_solve(lower, identity, left_side=True, lower=True)


def summed(partial_term):
    return lax.psum(partial_term, "rows")


def general(columns):
    col_count = lax.axis_size("cols")
    col_index = lax.axis_index("cols")
    scaling = math.sqrt(columns.shape[1] * lax.axis_size("rows"))
    local_rows = lax.all_gather(columns, "cols", axis=0, tiled=True)
    panel_count = 2 * PANEL
    leading = local_rows[:panel_count]
    gram_strip = summed(product(leading, local_rows.T))
    lower_both = jnp.linalg.cholesky(gram_strip[:, :panel_count])
    inverse_both = inverse_lower(lower_both)
    orthonormal = product(inverse_both, leading)
    coupling = product(inverse_both, gram_strip[:, panel_count:])
    trailing = local_rows[panel_count:] - product(coupling.T, orthonormal)
    triangle = jnp.concatenate([lower_both.T, coupling], axis=1)
    orthonormal = orthonormal * scaling
    triangle = triangle / scaling

    def own(array):
        count = array.shape[0] // col_count
        return lax.dynamic_slice_in_dim(array, col_index * count, count, 0)

    return (own(orthonormal), own(triangle), own(trailing))


def shards(columns):
    rows = lax.axis_size("rows")
    paired = lax.axis_size("cols") == 2 and columns.shape[0] == 2 * PANEL and columns.shape[1] % (8 * PANEL) == 0
    if paired and rows % 2 == 0 and (2 * PANEL) % (8 * rows) == 0 and (3 * PANEL) % (8 * rows) == 0:
        return fused(columns)
    return general(columns)


def solution(mesh):
    placed = (P("cols", "rows"),)
    return jax.shard_map(
        shards,
        mesh=mesh,
        in_specs=placed,
        out_specs=(P("cols", "rows"), P("cols", None), P("cols", "rows")),
        check_vma=False,
    )
```

profile of v0, /device:TPU:0, one launch (start us, length us, event | category | flops | bytes accessed | tf_op | source)
XLA Modules:
  0.0 40.7 jit_solution(1021343798852764630)
XLA Ops:
  0.6 0.0 copy-start
  0.6 1.2 %copy-done = f32[256,1024]{1,0:T(8,128)S(1)} copy-done((f32[256,1024]{1,0:T(8,128)S(1)}, f32[256,1024]{1,0:T(8,128)}, u32[]{:S(2)}) %copy-start) | copy-done | bytes 1048600
  1.9 36.9 %shard_map.38 = (f32[256,1024]{1,0:T(8,128)S(1)}, f32[128,512]{1,0:T(8,128)S(1)}, f32[128,1024]{1,0:T(8,128)S(1)}, f32[256,128]{1,0:T(8,128)S(1)}) custom-call(f32[256,1024]{1,0:T(8,128)S(1)} %copy-done), custom_call_target="tpu_custom_call" | custom-call | tf_op jit(solution)/shard_map/pallas_call | solution.py:361
  38.7 2.0 %shard_map.39 = (f32[128,1024]{1,0:T(8,128)}, f32[128,512]{1,0:T(8,128)}, f32[128,1024]{1,0:T(8,128)}) custom-call(f32[256,1024]{1,0:T(8,128)S(1)} %get-tuple-element.7.q_ref, f32[128,512]{1,0:T(8,128)S(1)} %get-tuple-element.8.tri_in, f32[128,1024]{1,0:T(8,128)S(1)} %get-tuple-element.9.tail_in, f32[256,128]{1,0:T(8,128)S(1)} %get-tuple-element.10.coup_ref), custom_call_target="tpu_custom_call" | custom-call | tf_op jit(solution)/shard_map/pallas_call | solution.py:406
Async XLA Ops:
  0.6 1.2 %copy-start = (f32[256,1024]{1,0:T(8,128)S(1)}, f32[256,1024]{1,0:T(8,128)}, u32[]{:S(2)}) copy-start(f32[256,1024]{1,0:T(8,128)} %x_ref.1) | copy-start | bytes 3145732
where the time goes:
time: 40.9 us; the launch traced here: 40.7 us
  Pallas kernels  38.9 us (95%)
  local copies, waits for them, and re-layouts  1.22 us (3%)
  between operations  0.65 us (2%)
    pallas_call x1, Pallas kernels, fused(): pl.pallas_call(functools.partial(kernel, row_count, scaling), out_shape=(...  36.9 us
    pallas_call x1, Pallas kernels, fused(): pl.pallas_call(functools.partial(finish_kernel, scaling), grid=(steps,),...  1.97 us
    unnamed x2, local copies, waits for them, and re-layouts  1.22 us

commit v1 on v0

v1 whole, which is shorter than its diff:
```python
import functools
import math

import jax
import jax.numpy as jnp
from jax import lax
from jax.experimental import pallas as pl
from jax.experimental.pallas import tpu as pltpu
from jax.sharding import PartitionSpec as P

PANEL = 128
STRIP = 16
VMEM_BYTES = 20 * 2**20
MESH = pl.DeviceIdType.MESH

precise = lax.Precision.HIGHEST


def product(left, right):
    return jnp.dot(left, right, precision=precise, preferred_element_type=jnp.float32)


def contract(left, right, dims):
    return lax.dot_general(
        left, right, (dims, ((), ())), precision=precise, preferred_element_type=jnp.float32
    )


def across_rows(left, right):
    return contract(left, right, ((1,), (1,)))


def pieces(value):
    first = value.astype(jnp.bfloat16)
    rest = value - first.astype(jnp.float32)
    second = rest.astype(jnp.bfloat16)
    third = (rest - second.astype(jnp.float32)).astype(jnp.bfloat16)
    return first, second, third


def strip_update(left, right):
    a, b, c = pieces(left)
    d, e, f = pieces(right)
    lhs = jnp.concatenate([a, a, b, a, c, b], axis=0)
    rhs = jnp.concatenate([d, e, d, f, d, e], axis=0)
    return lax.dot_general(
        lhs, rhs, (((0,), (0,)), ((), ())), preferred_element_type=jnp.float32
    )


def eliminate(ref, hooks):
    size = ref.shape[0]
    lanes = size
    parts = ref.shape[1] // lanes
    below = lax.broadcasted_iota(jnp.int32, (STRIP, lanes), 0)
    for s in range(size // STRIP):
        at = s * STRIP
        rows = [ref[at:at + STRIP, q * lanes:(q + 1) * lanes] for q in range(parts)]
        cols = [
            jnp.broadcast_to(rows[0][:, at + j:at + j + 1], (STRIP, lanes))
            for j in range(STRIP)
        ]
        for i in range(STRIP):
            pivot = cols[i][i:i + 1]
            inv = lax.rsqrt(pivot)
            inv = inv * (1.5 - 0.5 * pivot * inv * inv)
            col = cols[i] * inv
            coef = jnp.where(below > i, col, 0.0)
            for j in range(i + 1, STRIP):
                cols[j] = cols[j] - coef * col[j:j + 1]
            for q in range(parts):
                row = rows[q][i:i + 1] * inv
                rows[q] = jnp.where(below == i, row, rows[q] - coef * row)
        for q in range(parts):
            ref[at:at + STRIP, q * lanes:(q + 1) * lanes] = rows[q]
        after = at + STRIP
        if after < size:
            update = strip_update(rows[0], jnp.concatenate(rows, axis=1))
            ref[after:, :] = ref[after:, :] - update[after:, :]
        if s in hooks:
            hooks[s]()


def kernel(row_count, scaling, x_ref, q_ref, tail_ref, tri_ref, inv_ref, sum_ref,
           xs, ys, part, gram, pair_in, ring_in, first, second, inverse, power, z_ref,
           xy, xy_pair, xy_ring, xy_all, load, x_send, x_recv, g_send, g_recv,
           y_send, y_recv, relay):
    r = lax.axis_index("rows")
    c = lax.axis_index("cols")
    other = 1 - c
    parity = lax.rem(r, 2)
    h = r // 2
    mates = row_count // 2
    line = mates // 2
    place = h // 2
    partner = (r + 1 - 2 * parity, c)
    across = (r, other)
    side = ((h + 1 - 2 * lax.rem(h, 2)) * 2 + parity, c)
    above = (r + 4, c)
    below = (r - 4, c)
    has_above = place < line - 1
    has_below = place > 0
    size = PANEL
    width = xs.shape[1]
    half_width = width // 2
    eighth = width // 8

    def mate(k):
        return lax.rem(h + k, mates)

    def sender(k):
        return lax.rem(h + mates - k, mates)

    def at(idx, plane):
        return (idx * 2 + parity, plane)

    def push(src, dst, send_sem, recv_sem, target):
        return pltpu.make_async_remote_copy(
            src_ref=src, dst_ref=dst, send_sem=send_sem, recv_sem=recv_sem,
            device_id=target, device_id_type=MESH)

    def signal(sem, target):
        pl.semaphore_signal(sem, inc=1, device_id=target, device_id_type=MESH)

    barrier = pltpu.get_barrier_semaphore()
    for target in (across, partner, side):
        signal(barrier, target)

    @pl.when(has_above)
    def _():
        signal(barrier, above)

    @pl.when(has_below)
    def _():
        signal(barrier, below)

    early = pl.ds(0, half_width)
    late = pl.ds(half_width, half_width)

    def load_copy(q, dst):
        span = early if q == 0 else late
        return pltpu.make_async_copy(x_ref.at[:, span], dst.at[:, span], load.at[q])

    @pl.when(c == 0)
    def _():
        for q in range(2):
            load_copy(q, xs).start()

    @pl.when(c == 1)
    def _():
        for q in range(2):
            load_copy(q, ys).start()

    pl.semaphore_wait(barrier, 3 + has_above.astype(jnp.int32) + has_below.astype(jnp.int32))

    part_rows = size // 2
    top = [pl.ds(q * size, part_rows) for q in range(2)]
    bottom = [pl.ds(q * size + part_rows, part_rows) for q in range(2)]
    every = pl.ds(0, 2 * size)

    def cols(lo, count):
        return pl.ds(lo * eighth, count * eighth)

    x_views = (
        [(rows, late) for rows in top]
        + [(rows, cols(4, 2)) for rows in bottom]
        + [(rows, cols(6, 2)) for rows in bottom]
        + [(every, cols(0, 1)), (pl.ds(0, size), cols(1, 1)), (pl.ds(size, size), cols(1, 1)),
           (every, cols(2, 1)), (every, cols(3, 1))]
    )
    y_views = [(pl.ds(0, size), early), (pl.ds(size, size), early), (pl.ds(0, size), late)]

    def x_copy(q):
        return push(x_ref.at[x_views[q]], xs.at[x_views[q]], x_send.at[q], x_recv.at[q], across)

    def y_copy(q):
        return push(x_ref.at[y_views[q]], ys.at[y_views[q]], x_send.at[q], x_recv.at[q], across)

    @pl.when(c == 0)
    def _():
        for q in range(4):
            x_copy(q).start()

    @pl.when(c == 1)
    def _():
        for q in range(3):
            y_copy(q).start()

    @pl.when(jnp.logical_not(has_below))
    def _():
        signal(relay.at[0], above)

    @pl.when(jnp.logical_not(has_above))
    def _():
        signal(relay.at[1], below)

    def everyone():
        @pl.when(has_above)
        def _():
            pl.semaphore_wait(relay.at[1], 1)

        @pl.when(has_above & has_below)
        def _():
            signal(relay.at[1], below)

        @pl.when(has_below)
        def _():
            pl.semaphore_wait(relay.at[0], 1)

        @pl.when(has_below & has_above)
        def _():
            signal(relay.at[0], above)

        signal(relay.at[2], across)

    half = part.shape[0] // 2
    chunk = half // mates
    mine = pl.ds(parity * half, half)
    his = pl.ds((1 - parity) * half, half)

    def piece(idx):
        return pl.ds(pl.multiple_of(parity * half + idx * chunk, 8), chunk)

    own = piece(h)

    def g_pair():
        return push(part.at[his], pair_in, g_send.at[0], g_recv.at[0], partner)

    def g_ring(k):
        return push(part.at[piece(mate(k))], ring_in.at[k], g_send.at[k],
                    g_recv.at[k], at(mate(k), c))

    def g_cross():
        return push(gram.at[own], gram.at[own], g_send.at[mates], g_recv.at[mates], across)

    def g_gather(k, idx):
        return push(gram.at[piece(idx)], gram.at[piece(idx)], g_send.at[mates + k],
                    g_recv.at[mates + k], at(mate(k), c))

    def g_half(rows):
        return push(gram.at[rows], gram.at[rows], g_send.at[2 * mates],
                    g_recv.at[2 * mates], partner)

    first_owner = mates // 4
    owners = range(first_owner, mates - first_owner)
    split = mates // 2
    rows_chunk = size // len(owners)
    is_owner = (h >= first_owner) & (h < mates - first_owner)

    def rows_at(offset, count):
        return pl.ds(pl.multiple_of(offset, 8), count)

    y_mine = rows_at(parity * size, size)
    y_his = rows_at((1 - parity) * size, size)

    def y_piece(idx):
        return rows_at(parity * size + (idx - first_owner) * rows_chunk, rows_chunk)

    def y_pair(q):
        if q < 2:
            src, dst = xy.at[q, y_his], xy_pair.at[q]
        else:
            rows = rows_at((1 - parity) * size + (q - 2) * part_rows, part_rows)
            src, dst = xy.at[:, rows], xy_pair.at[:, pl.ds((q - 2) * part_rows, part_rows)]
        return push(src, dst, y_send.at[q % 2], y_recv.at[q % 2], partner)

    def y_merge(q):
        if q < 2:
            xy[q, y_mine] = xy[q, y_mine] + xy_pair[q]
        else:
            rows = rows_at(parity * size + (q - 2) * part_rows, part_rows)
            span = pl.ds((q - 2) * part_rows, part_rows)
            xy[:, rows] = xy[:, rows] + xy_pair[:, span]

    near, far, share, lend, final = (2 + k * mates for k in range(5))

    def y_near(j):
        return push(xy.at[c, y_piece(j)], xy_ring.at[0, h], y_send.at[near + j],
                    y_recv.at[near + h], at(j, c))

    def y_far(j):
        return push(xy.at[other, y_piece(j)], xy_ring.at[1, h], y_send.at[far + j],
                    y_recv.at[far + h], at(j, other))

    def y_arrive(which, j):
        base = (near, far)[which]
        return push(xy_ring.at[which, j], xy_ring.at[which, j], y_send.at[base + j],
                    y_recv.at[base + j], at(j, c))

    def y_share(j):
        view = xy_all.at[c, y_piece(h)]
        return push(view, view, y_send.at[share + j], y_recv.at[share + h], at(j, c))

    def y_lend(j):
        view = xy_all.at[c, y_piece(h)]
        return push(view, view, y_send.at[lend + j], y_recv.at[lend + h], at(j, other))

    def y_result(which, j):
        base, plane = ((share, c), (lend, other))[which]
        view = xy_all.at[plane, y_piece(j)]
        return push(view, view, y_send.at[base + j], y_recv.at[base + j], at(j, plane))

    def y_half(which, plane, rows):
        view = xy_all.at[plane, rows]
        return push(view, view, y_send.at[final + which], y_recv.at[final + which], partner)

    def unless_self(j, step):
        @pl.when(h != j)
        def _():
            step()

    def scatter(q):
        y_pair(q).wait_recv()
        y_merge(q)
        targets = owners if q < 2 else [j for j in owners if (j >= split) == (q == 3)]
        if q != 0:
            for j in targets:
                y_far(j).start()
        if q != 1:
            for j in targets:
                unless_self(j, y_near(j).start)

    def meet(q):
        if q < 2:
            xy[q] = across_rows(xs[:, early], ys[q * size:(q + 1) * size, early])
        else:
            groups = (top, bottom)[q - 2]
            value = across_rows(
                jnp.concatenate([xs[rows, late] for rows in groups], axis=0), ys[:, late])
            for g, rows in enumerate(groups):
                block = value[g * part_rows:(g + 1) * part_rows]
                xy[0, rows] = block[:, :size]
                xy[1, rows] = block[:, size:]
        y_pair(q).start()

    @pl.when(c == 0)
    def _():
        for q in range(2):
            load_copy(q, xs).wait()
            span = early if q == 0 else late
            strip = across_rows(xs[:size, span], xs[:, span])
            rest = across_rows(xs[size:, span], xs[size:, span])
            if q == 0:
                part[:size] = strip[:, :size]
                part[size:2 * size] = strip[:, size:]
                part[2 * size:] = rest
            else:
                part[:size] = part[:size] + strip[:, :size]
                part[size:2 * size] = part[size:2 * size] + strip[:, size:]
                part[2 * size:] = part[2 * size:] + rest
        g_pair().start()

    everyone()

    @pl.when(c == 0)
    def _():
        g_pair().wait_recv()
        part[mine] = part[mine] + pair_in[...]
        for k in range(1, mates):
            g_ring(k).start()
        for k in range(1, mates):
            g_ring(k).wait_recv()
        total = part[own]
        for k in range(1, mates):
            total = total + ring_in[k]
        gram[own] = total
        g_cross().start()
        for q in range(4, 7):
            x_copy(q).start()

    @pl.when(c == 1)
    def _():
        for q in range(2):
            load_copy(q, ys).wait()
        for q in range(2):
            x_copy(q).wait_recv()
        meet(2)
        pl.semaphore_wait(relay.at[2], 1)
        scatter(2)
        g_cross().wait_recv()

    for k in range(1, mates):
        g_gather(k, h).start()

    @pl.when(c == 0)
    def _():
        y_copy(0).wait_recv()
        meet(0)

    @pl.when(c == 1)
    def _():
        for q in range(2, 6):
            x_copy(q).wait_recv()
        meet(3)

    for k in range(1, mates):
        g_gather(k, sender(k)).wait_recv()
    g_half(mine).start()

    @pl.when(c == 0)
    def _():
        scatter(0)

    @pl.when(c == 1)
    def _():
        scatter(3)

    g_half(his).wait_recv()

    eye = (lax.broadcasted_iota(jnp.int32, (size, size), 0)
           == lax.broadcasted_iota(jnp.int32, (size, size), 1)).astype(jnp.float32)
    first[:, :size] = gram[:size]
    first[:, size:2 * size] = gram[size:2 * size]
    first[:, 2 * size:] = eye

    def on_plane(plane, step):
        @pl.when(c == plane)
        def _():
            step()

    def meet_last():
        y_copy(1).wait_recv()
        x_copy(7).start()
        meet(1)

    def scatter_last():
        pl.semaphore_wait(relay.at[2], 1)
        scatter(1)
        for q in range(8, 10):
            x_copy(q).start()

    def gather():
        @pl.when(is_owner)
        def _():
            for j in range(mates):
                unless_self(j, y_arrive(0, j).wait_recv)
            for j in range(mates):
                y_arrive(1, j).wait_recv()
            total = xy[c, y_piece(h)]
            for k in range(1, mates):
                total = total + xy_ring[0, mate(k)]
            for j in range(mates):
                total = total + xy_ring[1, j]
            xy_all[c, y_piece(h)] = total
            for j in range(mates):
                unless_self(j, y_share(j).start)
            for j in range(mates):
                y_lend(j).start()

        @pl.when(c == 0)
        def _():
            x_copy(10).start()

    eliminate(first, {
        1: lambda: on_plane(0, meet_last),
        3: lambda: on_plane(0, scatter_last),
    })

    upper = first[:, size:2 * size]
    cross = contract(upper, first[:, size:], ((0,), (0,)))
    second[:, :size] = gram[2 * size:] - cross[:, :size]
    second[:, size:2 * size] = -cross[:, size:]
    second[:, 2 * size:] = eye
    eliminate(second, {
        1: lambda: on_plane(1, gather),
        4: lambda: on_plane(0, gather),
    })

    inverse[:size, :size] = first[:, 2 * size:]
    inverse[:size, size:] = jnp.zeros((size, size), jnp.float32)
    inverse[size:] = second[:, size:]
    power[...] = contract(inverse[...], inverse[...], ((0,), (0,)))
    own_rows = pl.ds(pl.multiple_of(c * size, size), size)

    def products(lo, count):
        span = pl.ds(lo * eighth, count * eighth)
        q_ref[:, span] = product(inverse[own_rows], xs[:, span]) * scaling
        z_ref[:, span] = product(power[...], xs[:, span])

    keep = (lax.broadcasted_iota(jnp.int32, (size, size), 0)
            <= lax.broadcasted_iota(jnp.int32, (size, size), 1))

    def trail(lo, count):
        span = cols(lo, count)
        tail_ref[:, span] = ys[own_rows, span] - contract(
            xy_all[c], z_ref[:, span], ((0,), (0,)))

    @pl.when(c == 0)
    def _():
        tri_ref[:, :size] = jnp.where(keep, first[:, :size], 0.0) / scaling
        tri_ref[:, size:2 * size] = first[:, size:2 * size] / scaling
        y_copy(2).wait_recv()

    @pl.when(c == 1)
    def _():
        tri_ref[:, :size] = jnp.zeros((size, size), jnp.float32)
        tri_ref[:, size:2 * size] = jnp.where(keep, second[:, :size], 0.0) / scaling
        x_copy(6).wait_recv()

    inv_ref[...] = inverse[own_rows]
    products(4, 4)
    products(0, 1)

    @pl.when(c == 1)
    def _():
        for q in range(7, 10):
            x_copy(q).wait_recv()

    products(1, 2)

    @pl.when(c == 0)
    def _():
        products(3, 1)
        for q in range(10):
            x_copy(q).wait_send()
        g_pair().wait_send()
        for k in range(1, mates):
            g_ring(k).wait_send()
        g_cross().wait_send()
        for q in range(2):
            y_pair(q).wait_send()

    @pl.when(c == 1)
    def _():
        for q in range(len(y_views)):
            y_copy(q).wait_send()
        for q in range(2, 4):
            y_pair(q).wait_send()

    for k in range(1, mates):
        g_gather(k, h).wait_send()
    g_half(mine).wait_send()
    for j in owners:
        unless_self(j, y_near(j).wait_send)
        y_far(j).wait_send()

    for j in owners:
        unless_self(j, y_result(0, j).wait_recv)
    y_half(0, c, y_mine).start()
    for j in owners:
        y_result(1, j).wait_recv()
    y_half(1, other, y_mine).start()
    y_half(0, c, y_his).wait_recv()
    trail(4, 4)
    trail(0, 3)
    sum_ref[c] = xy_all[c]

    @pl.when(is_owner)
    def _():
        for j in range(mates):
            unless_self(j, y_share(j).wait_send)
            y_lend(j).wait_send()

    @pl.when(c == 1)
    def _():
        x_copy(10).wait_recv()
        products(3, 1)

    @pl.when(c == 0)
    def _():
        x_copy(10).wait_send()

    trail(3, 1)
    y_half(1, other, y_his).wait_recv()
    sum_ref[other] = xy_all[other]
    y_half(0, c, y_mine).wait_send()
    y_half(1, other, y_mine).wait_send()


def finish_kernel(scaling, q_in, tail_in, tri_in, inv_ref, sum_ref,
                  ortho_ref, tri_ref, trail_ref, right, sems):
    size = tri_in.shape[0]

    def out(k, src, dst):
        return pltpu.make_async_copy(src, dst, sems.at[k])

    copies = [
        out(0, q_in, ortho_ref),
        out(1, tail_in, trail_ref),
        out(2, tri_in, tri_ref.at[:, :2 * size]),
        out(3, right, tri_ref.at[:, 2 * size:]),
    ]
    for copy in copies[:3]:
        copy.start()
    right[:, :size] = product(inv_ref[...], sum_ref[0]) / scaling
    right[:, size:] = product(inv_ref[...], sum_ref[1]) / scaling
    copies[3].start()
    for copy in copies:
        copy.wait()


def fused(columns):
    row_count = lax.axis_size("rows")
    width = columns.shape[1]
    scaling = math.sqrt(width * row_count)
    size = PANEL
    mates = row_count // 2
    f32 = jnp.float32
    vmem = pl.BlockSpec(memory_space=pltpu.VMEM)
    ortho = jax.ShapeDtypeStruct((size, width), f32)
    triangle = jax.ShapeDtypeStruct((size, 4 * size), f32)
    trailing = ortho
    middle = pl.pallas_call(
        functools.partial(kernel, row_count, scaling),
        out_shape=(
            ortho,
            trailing,
            jax.ShapeDtypeStruct((size, 2 * size), f32),
            jax.ShapeDtypeStruct((size, 2 * size), f32),
            jax.ShapeDtypeStruct((2, 2 * size, size), f32),
        ),
        in_specs=[pl.BlockSpec(memory_space=pltpu.HBM)],
        out_specs=(vmem,) * 5,
        scratch_shapes=[
            pltpu.VMEM((2 * size, width), f32),
            pltpu.VMEM((2 * size, width), f32),
            pltpu.VMEM((3 * size, size), f32),
            pltpu.VMEM((3 * size, size), f32),
            pltpu.VMEM((3 * size // 2, size), f32),
            pltpu.VMEM((mates, 3 * size // row_count, size), f32),
            pltpu.VMEM((size, 3 * size), f32),
            pltpu.VMEM((size, 3 * size), f32),
            pltpu.VMEM((2 * size, 2 * size), f32),
            pltpu.VMEM((2 * size, 2 * size), f32),
            pltpu.VMEM((2 * size, width), f32),
            pltpu.VMEM((2, 2 * size, size), f32),
            pltpu.VMEM((2, size, size), f32),
            pltpu.VMEM((2, mates, size // (mates // 2), size), f32),
            pltpu.VMEM((2, 2 * size, size), f32),
            pltpu.SemaphoreType.DMA((2,)),
            pltpu.SemaphoreType.DMA((11,)),
            pltpu.SemaphoreType.DMA((11,)),
            pltpu.SemaphoreType.DMA((2 * mates + 1,)),
            pltpu.SemaphoreType.DMA((2 * mates + 1,)),
            pltpu.SemaphoreType.DMA((4 * mates + 4,)),
            pltpu.SemaphoreType.DMA((4 * mates + 4,)),
            pltpu.SemaphoreType.REGULAR((3,)),
        ],
        compiler_params=pltpu.CompilerParams(
            collective_id=0, has_side_effects=True, vmem_limit_bytes=VMEM_BYTES),
    )(pltpu.with_memory_space_constraint(columns, pltpu.HBM))
    return pl.pallas_call(
        functools.partial(finish_kernel, scaling),
        out_shape=(ortho, triangle, trailing),
        in_specs=[vmem] * 5,
        out_specs=(pl.BlockSpec(memory_space=pltpu.HBM),) * 3,
        scratch_shapes=[
            pltpu.VMEM((size, 2 * size), f32),
            pltpu.SemaphoreType.DMA((4,)),
        ],
        compiler_params=pltpu.CompilerParams(vmem_limit_bytes=VMEM_BYTES),
    )(*middle)


def inverse_lower(lower):
    identity = jnp.eye(lower.shape[0], dtype=lower.dtype)
    return lax.linalg.triangular_solve(lower, identity, left_side=True, lower=True)


def summed(partial_term):
    return lax.psum(partial_term, "rows")


def general(columns):
    col_count = lax.axis_size("cols")
    col_index = lax.axis_index("cols")
    scaling = math.sqrt(columns.shape[1] * lax.axis_size("rows"))
    local_rows = lax.all_gather(columns, "cols", axis=0, tiled=True)
    panel_count = 2 * PANEL
    leading = local_rows[:panel_count]
    gram_strip = summed(product(leading, local_rows.T))
    lower_both = jnp.linalg.cholesky(gram_strip[:, :panel_count])
    inverse_both = inverse_lower(lower_both)
    orthonormal = product(inverse_both, leading)
    coupling = product(inverse_both, gram_strip[:, panel_count:])
    trailing = local_rows[panel_count:] - product(coupling.T, orthonormal)
    triangle = jnp.concatenate([lower_both.T, coupling], axis=1)
    orthonormal = orthonormal * scaling
    triangle = triangle / scaling

    def own(array):
        count = array.shape[0] // col_count
        return lax.dynamic_slice_in_dim(array, col_index * count, count, 0)

    return (own(orthonormal), own(triangle), own(trailing))


def shards(columns):
    rows = lax.axis_size("rows")
    paired = lax.axis_size("cols") == 2 and columns.shape[0] == 2 * PANEL and columns.shape[1] % (8 * PANEL) == 0
    if paired and rows % 8 == 0 and (2 * PANEL) % (8 * rows) == 0 and (3 * PANEL) % (8 * rows) == 0:
        return fused(columns)
    return general(columns)


def solution(mesh):
    placed = (P("cols", "rows"),)
    return jax.shard_map(
        shards,
        mesh=mesh,
        in_specs=placed,
        out_specs=(P("cols", "rows"), P("cols", None), P("cols", "rows")),
        check_vma=False,
    )
```

time: 40.9 us -> 37.1 us (0.907)
  Pallas kernels: 38.9 us -> 36 us
  local copies, waits for them, and re-layouts: 1.22 us -> 0 us
    pallas_call x1, Pallas kernels: 36.9 us -> 34.9 us  [fused(): pl.pallas_call(functools.partial(kernel, row_count, scaling), out_shape=(...]
    unnamed x2 -> x0, local copies, waits for them, and re-layouts: 1.22 us -> none
    pallas_call x1, Pallas kernels: 1.97 us -> 1.08 us  [fused(): pl.pallas_call(functools.partial(finish_kernel, scaling), out_shape=(orth...]
where the time goes in v1:
time: 37.1 us; the launch traced here: 36.7 us
  Pallas kernels  36 us (97%)
  between operations  0.64 us (2%)
    pallas_call x1, Pallas kernels, fused(): pl.pallas_call(functools.partial(kernel, row_count, scaling), out_shape=(...  34.9 us
    pallas_call x1, Pallas kernels, fused(): pl.pallas_call(functools.partial(finish_kernel, scaling), out_shape=(orth...  1.08 us

profile of v1, /device:TPU:0, one launch (start us, length us, event | category | flops | bytes accessed | tf_op | source)
XLA Modules:
  0.0 36.7 jit_solution(16971189403813360613)
XLA Ops:
  0.6 34.9 %shard_map.38 = (f32[128,1024]{1,0:T(8,128)S(1)}, f32[128,1024]{1,0:T(8,128)S(1)}, f32[128,256]{1,0:T(8,128)S(1)}, f32[128,256]{1,0:T(8,128)S(1)}, f32[2,256,128]{2,1,0:T(8,128)S(1)}) custom-call(f32[256,1024]{1,0:T(8,128)} %x_ref.1), custom_call_target="tpu_custom_call" | custom-call | tf_op jit(solution)/shard_map/pallas_call | solution.py:603
  35.6 1.1 %shard_map.39 = (f32[128,1024]{1,0:T(8,128)}, f32[128,512]{1,0:T(8,128)}, f32[128,1024]{1,0:T(8,128)}) custom-call(f32[128,1024]{1,0:T(8,128)S(1)} %get-tuple-element.8.q_in, f32[128,1024]{1,0:T(8,128)S(1)} %get-tuple-element.9.tail_in, f32[128,256]{1,0:T(8,128)S(1)} %get-tuple-element.10.tri_in, f32[128,256]{1,0:T(8,128)S(1)} %get-tuple-element.11.inv_ref, ...), custom_call_target="tpu_custom_call" | custom-call | tf_op jit(solution)/shard_map/pallas_call | solution.py:642

commit v2 on v1

--- a/solution.py
+++ b/solution.py
@@ -38,14 +38,17 @@
     return first, second, third
 
 
-def strip_update(left, right):
+def strip_update(left, right, after):
     a, b, c = pieces(left)
     d, e, f = pieces(right)
     lhs = jnp.concatenate([a, a, b, a, c, b], axis=0)
     rhs = jnp.concatenate([d, e, d, f, d, e], axis=0)
-    return lax.dot_general(
-        lhs, rhs, (((0,), (0,)), ((), ())), preferred_element_type=jnp.float32
-    )
+    return jnp.dot(lhs.T[after:], rhs, preferred_element_type=jnp.float32)
+
+
+def root_inverse(value):
+    guess = lax.rsqrt(value)
+    return guess * (1.5 - (0.5 * value) * guess * guess)
 
 
 def eliminate(ref, hooks):
@@ -60,23 +63,33 @@
             jnp.broadcast_to(rows[0][:, at + j:at + j + 1], (STRIP, lanes))
             for j in range(STRIP)
         ]
-        for i in range(STRIP):
-            pivot = cols[i][i:i + 1]
-            inv = lax.rsqrt(pivot)
-            inv = inv * (1.5 - 0.5 * pivot * inv * inv)
+        scales = [lax.rsqrt(cols[i][i:i + 1]) for i in range(0, STRIP, 2)]
+        for i in range(0, STRIP, 2):
+            scale = scales[i // 2]
+            corner = cols[i][i:i + 1]
+            edge = cols[i][i + 1:i + 2]
+            unit = corner * scale * scale
+            minor = unit * cols[i + 1][i + 1:i + 2] - edge * scale * scale * edge
+            inv = root_inverse(corner)
+            inv_next = root_inverse(minor) * (unit * root_inverse(unit))
             col = cols[i] * inv
+            col_next = (cols[i + 1] - col * col[i + 1:i + 2]) * inv_next
             coef = jnp.where(below > i, col, 0.0)
-            for j in range(i + 1, STRIP):
-                cols[j] = cols[j] - coef * col[j:j + 1]
+            coef_next = jnp.where(below > i + 1, col_next, 0.0)
+            for j in range(i + 2, STRIP):
+                cols[j] = cols[j] - coef * col[j:j + 1] - coef_next * col_next[j:j + 1]
             for q in range(parts):
                 row = rows[q][i:i + 1] * inv
-                rows[q] = jnp.where(below == i, row, rows[q] - coef * row)
+                rest = rows[q] - coef * row
+                row_next = rest[i + 1:i + 2] * inv_next
+                rest = jnp.where(below == i + 1, row_next, rest - coef_next * row_next)
+                rows[q] = jnp.where(below == i, row, rest)
         for q in range(parts):
             ref[at:at + STRIP, q * lanes:(q + 1) * lanes] = rows[q]
         after = at + STRIP
         if after < size:
-            update = strip_update(rows[0], jnp.concatenate(rows, axis=1))
-            ref[after:, :] = ref[after:, :] - update[after:, :]
+            update = strip_update(rows[0], jnp.concatenate(rows, axis=1), after)
+            ref[after:, :] = ref[after:, :] - update
         if s in hooks:
             hooks[s]()
 
@@ -108,9 +121,6 @@
     def mate(k):
         return lax.rem(h + k, mates)
 
-    def sender(k):
-        return lax.rem(h + mates - k, mates)
-
     def at(idx, plane):
         return (idx * 2 + parity, plane)
 
@@ -170,11 +180,33 @@
     )
     y_views = [(pl.ds(0, size), early), (pl.ds(size, size), early), (pl.ds(0, size), late)]
 
+    x_group = (0, 0, 1, 1, 1, 1, 2, 3, 3, 3, 4)
+
     def x_copy(q):
-        return push(x_ref.at[x_views[q]], xs.at[x_views[q]], x_send.at[q], x_recv.at[q], across)
+        return push(x_ref.at[x_views[q]], xs.at[x_views[q]], x_send.at[0],
+                    x_recv.at[x_group[q]], across)
 
     def y_copy(q):
-        return push(x_ref.at[y_views[q]], ys.at[y_views[q]], x_send.at[q], x_recv.at[q], across)
+        return push(x_ref.at[y_views[q]], ys.at[y_views[q]], x_send.at[0], x_recv.at[q], across)
+
+    def bulk(ref, send_sem, recv_sem):
+        return push(ref, ref, send_sem, recv_sem, across)
+
+    x_sizes = ((size, late), (size, late), (2 * size, cols(0, 1)), (2 * size, cols(1, 2)),
+               (2 * size, cols(3, 1)))
+
+    def x_group_wait(g):
+        rows, span = x_sizes[g]
+        bulk(xs.at[pl.ds(0, rows), span], x_send.at[0], x_recv.at[g]).wait_recv()
+
+    def bulk_sent():
+        @pl.when(c == 0)
+        def _():
+            bulk(xs, x_send.at[0], x_recv.at[0]).wait_send()
+
+        @pl.when(c == 1)
+        def _():
+            bulk(ys.at[pl.ds(0, 3 * size // 2)], x_send.at[0], x_recv.at[0]).wait_send()
 
     @pl.when(c == 0)
     def _():
@@ -186,31 +218,38 @@
         for q in range(3):
             y_copy(q).start()
 
-    @pl.when(jnp.logical_not(has_below))
+    up_next = has_below & has_above
+    up_waits = place > 1
+    down_next = has_above & has_below
+    down_waits = place < line - 2
+
+    @pl.when(up_next & jnp.logical_not(up_waits))
     def _():
         signal(relay.at[0], above)
 
-    @pl.when(jnp.logical_not(has_above))
+    @pl.when(down_next & jnp.logical_not(down_waits))
     def _():
         signal(relay.at[1], below)
 
     def everyone():
-        @pl.when(has_above)
+        @pl.when(up_waits)
+        def _():
+            pl.semaphore_wait(relay.at[0], 1)
+
+        @pl.when(up_waits & up_next)
+        def _():
+            signal(relay.at[0], above)
+
+        @pl.when(down_waits)
         def _():
             pl.semaphore_wait(relay.at[1], 1)
 
-        @pl.when(has_above & has_below)
+        @pl.when(down_waits & down_next)
         def _():
             signal(relay.at[1], below)
 
-        @pl.when(has_below)
-        def _():
-            pl.semaphore_wait(relay.at[0], 1)
-
-        @pl.when(has_below & has_above)
-        def _():
-            signal(relay.at[0], above)
-
+        signal(relay.at[3], side)
+        pl.semaphore_wait(relay.at[3], 1)
         signal(relay.at[2], across)
 
     half = part.shape[0] // 2
@@ -227,19 +266,20 @@
         return push(part.at[his], pair_in, g_send.at[0], g_recv.at[0], partner)
 
     def g_ring(k):
-        return push(part.at[piece(mate(k))], ring_in.at[k], g_send.at[k],
-                    g_recv.at[k], at(mate(k), c))
+        return push(part.at[piece(mate(k))], ring_in.at[k], g_send.at[0],
+                    g_recv.at[1], at(mate(k), c))
 
     def g_cross():
-        return push(gram.at[own], gram.at[own], g_send.at[mates], g_recv.at[mates], across)
-
-    def g_gather(k, idx):
-        return push(gram.at[piece(idx)], gram.at[piece(idx)], g_send.at[mates + k],
-                    g_recv.at[mates + k], at(mate(k), c))
+        return push(gram.at[own], gram.at[own], g_send.at[0], g_recv.at[2], across)
+
+    def g_gather(k):
+        return push(gram.at[own], gram.at[own], g_send.at[1], g_recv.at[3], at(mate(k), c))
 
     def g_half(rows):
-        return push(gram.at[rows], gram.at[rows], g_send.at[2 * mates],
-                    g_recv.at[2 * mates], partner)
+        return push(gram.at[rows], gram.at[rows], g_send.at[1], g_recv.at[4], partner)
+
+    def amount(ref, send_sem, recv_sem):
+        return push(ref, ref, send_sem, recv_sem, partner)
 
     first_owner = mates // 4
     owners = range(first_owner, mates - first_owner)
@@ -262,7 +302,7 @@
         else:
             rows = rows_at((1 - parity) * size + (q - 2) * part_rows, part_rows)
             src, dst = xy.at[:, rows], xy_pair.at[:, pl.ds((q - 2) * part_rows, part_rows)]
-        return push(src, dst, y_send.at[q % 2], y_recv.at[q % 2], partner)
+        return push(src, dst, y_send.at[0], y_recv.at[q % 2], partner)
 
     def y_merge(q):
         if q < 2:
@@ -272,37 +312,36 @@
             span = pl.ds((q - 2) * part_rows, part_rows)
             xy[:, rows] = xy[:, rows] + xy_pair[:, span]
 
-    near, far, share, lend, final = (2 + k * mates for k in range(5))
+    near, far, share, lend, final = range(2, 7)
 
     def y_near(j):
-        return push(xy.at[c, y_piece(j)], xy_ring.at[0, h], y_send.at[near + j],
-                    y_recv.at[near + h], at(j, c))
+        return push(xy.at[c, y_piece(j)], xy_ring.at[0, h], y_send.at[1],
+                    y_recv.at[near], at(j, c))
 
     def y_far(j):
-        return push(xy.at[other, y_piece(j)], xy_ring.at[1, h], y_send.at[far + j],
-                    y_recv.at[far + h], at(j, other))
-
-    def y_arrive(which, j):
-        base = (near, far)[which]
-        return push(xy_ring.at[which, j], xy_ring.at[which, j], y_send.at[base + j],
-                    y_recv.at[base + j], at(j, c))
+        return push(xy.at[other, y_piece(j)], xy_ring.at[1, h], y_send.at[0],
+                    y_recv.at[far], at(j, other))
 
     def y_share(j):
         view = xy_all.at[c, y_piece(h)]
-        return push(view, view, y_send.at[share + j], y_recv.at[share + h], at(j, c))
+        return push(view, view, y_send.at[2], y_recv.at[share], at(j, c))
 
     def y_lend(j):
         view = xy_all.at[c, y_piece(h)]
-        return push(view, view, y_send.at[lend + j], y_recv.at[lend + h], at(j, other))
-
-    def y_result(which, j):
-        base, plane = ((share, c), (lend, other))[which]
-        view = xy_all.at[plane, y_piece(j)]
-        return push(view, view, y_send.at[base + j], y_recv.at[base + j], at(j, plane))
+        return push(view, view, y_send.at[3], y_recv.at[lend], at(j, other))
 
     def y_half(which, plane, rows):
         view = xy_all.at[plane, rows]
-        return push(view, view, y_send.at[final + which], y_recv.at[final + which], partner)
+        return push(view, view, y_send.at[4], y_recv.at[final + which], partner)
+
+    def by_role(count, step):
+        @pl.when(is_owner)
+        def _():
+            step(count - 1)
+
+        @pl.when(jnp.logical_not(is_owner))
+        def _():
+            step(count)
 
     def unless_self(j, step):
         @pl.when(h != j)
@@ -358,8 +397,7 @@
         part[mine] = part[mine] + pair_in[...]
         for k in range(1, mates):
             g_ring(k).start()
-        for k in range(1, mates):
-            g_ring(k).wait_recv()
+        amount(ring_in.at[pl.ds(1, mates - 1)], g_send.at[0], g_recv.at[1]).wait_recv()
         total = part[own]
         for k in range(1, mates):
             total = total + ring_in[k]
@@ -372,15 +410,14 @@
     def _():
         for q in range(2):
             load_copy(q, ys).wait()
-        for q in range(2):
-            x_copy(q).wait_recv()
+        x_group_wait(0)
         meet(2)
         pl.semaphore_wait(relay.at[2], 1)
         scatter(2)
         g_cross().wait_recv()
 
     for k in range(1, mates):
-        g_gather(k, h).start()
+        g_gather(k).start()
 
     @pl.when(c == 0)
     def _():
@@ -389,21 +426,16 @@
 
     @pl.when(c == 1)
     def _():
-        for q in range(2, 6):
-            x_copy(q).wait_recv()
+        x_group_wait(1)
         meet(3)
-
-    for k in range(1, mates):
-        g_gather(k, sender(k)).wait_recv()
+        scatter(3)
+
+    amount(gram.at[pl.ds(0, (mates - 1) * chunk)], g_send.at[1], g_recv.at[3]).wait_recv()
     g_half(mine).start()
 
     @pl.when(c == 0)
     def _():
         scatter(0)
-
-    @pl.when(c == 1)
-    def _():
-        scatter(3)
 
     g_half(his).wait_recv()
 
@@ -432,10 +464,8 @@
     def gather():
         @pl.when(is_owner)
         def _():
-            for j in range(mates):
-                unless_self(j, y_arrive(0, j).wait_recv)
-            for j in range(mates):
-                y_arrive(1, j).wait_recv()
+            amount(xy_ring.at[0, pl.ds(0, mates - 1)], y_send.at[1], y_recv.at[near]).wait_recv()
+            amount(xy_ring.at[1], y_send.at[0], y_recv.at[far]).wait_recv()
             total = xy[c, y_piece(h)]
             for k in range(1, mates):
                 total = total + xy_ring[0, mate(k)]
@@ -452,8 +482,8 @@
             x_copy(10).start()
 
     eliminate(first, {
-        1: lambda: on_plane(0, meet_last),
-        3: lambda: on_plane(0, scatter_last),
+        0: lambda: on_plane(0, meet_last),
+        2: lambda: on_plane(0, scatter_last),
     })
 
     upper = first[:, size:2 * size]
@@ -463,7 +493,7 @@
     second[:, 2 * size:] = eye
     eliminate(second, {
         1: lambda: on_plane(1, gather),
-        4: lambda: on_plane(0, gather),
+        3: lambda: on_plane(0, gather),
     })
 
     inverse[:size, :size] = first[:, 2 * size:]
@@ -495,7 +525,7 @@
     def _():
         tri_ref[:, :size] = jnp.zeros((size, size), jnp.float32)
         tri_ref[:, size:2 * size] = jnp.where(keep, second[:, :size], 0.0) / scaling
-        x_copy(6).wait_recv()
+        x_group_wait(2)
 
     inv_ref[...] = inverse[own_rows]
     products(4, 4)
@@ -503,42 +533,27 @@
 
     @pl.when(c == 1)
     def _():
-        for q in range(7, 10):
-            x_copy(q).wait_recv()
+        x_group_wait(3)
 
     products(1, 2)
 
     @pl.when(c == 0)
     def _():
         products(3, 1)
-        for q in range(10):
-            x_copy(q).wait_send()
-        g_pair().wait_send()
-        for k in range(1, mates):
-            g_ring(k).wait_send()
-        g_cross().wait_send()
-        for q in range(2):
-            y_pair(q).wait_send()
-
-    @pl.when(c == 1)
-    def _():
-        for q in range(len(y_views)):
-            y_copy(q).wait_send()
-        for q in range(2, 4):
-            y_pair(q).wait_send()
-
-    for k in range(1, mates):
-        g_gather(k, h).wait_send()
-    g_half(mine).wait_send()
-    for j in owners:
-        unless_self(j, y_near(j).wait_send)
-        y_far(j).wait_send()
-
-    for j in owners:
-        unless_self(j, y_result(0, j).wait_recv)
+        amount(part, g_send.at[0], g_recv.at[0]).wait_send()
+
+    amount(gram.at[pl.ds(0, (mates - 1) * chunk + half)], g_send.at[1], g_recv.at[0]).wait_send()
+    amount(part, y_send.at[0], y_recv.at[0]).wait_send()
+
+    def rows_of(count):
+        return xy_all.at[0, pl.ds(0, count * rows_chunk)]
+
+    by_role(len(owners), lambda n: amount(
+        rows_of(n), y_send.at[1], y_recv.at[0]).wait_send())
+    by_role(len(owners), lambda n: amount(
+        rows_of(n), y_send.at[1], y_recv.at[share]).wait_recv())
     y_half(0, c, y_mine).start()
-    for j in owners:
-        y_result(1, j).wait_recv()
+    amount(rows_of(len(owners)), y_send.at[1], y_recv.at[lend]).wait_recv()
     y_half(1, other, y_mine).start()
     y_half(0, c, y_his).wait_recv()
     trail(4, 4)
@@ -547,24 +562,19 @@
 
     @pl.when(is_owner)
     def _():
-        for j in range(mates):
-            unless_self(j, y_share(j).wait_send)
-            y_lend(j).wait_send()
+        amount(rows_of(mates - 1), y_send.at[2], y_recv.at[0]).wait_send()
+        amount(rows_of(mates), y_send.at[3], y_recv.at[0]).wait_send()
 
     @pl.when(c == 1)
     def _():
-        x_copy(10).wait_recv()
+        x_group_wait(4)
         products(3, 1)
 
-    @pl.when(c == 0)
-    def _():
-        x_copy(10).wait_send()
-
+    bulk_sent()
     trail(3, 1)
     y_half(1, other, y_his).wait_recv()
     sum_ref[other] = xy_all[other]
-    y_half(0, c, y_mine).wait_send()
-    y_half(1, other, y_mine).wait_send()
+    amount(xy_pair, y_send.at[4], y_recv.at[0]).wait_send()
 
 
 def finish_kernel(scaling, q_in, tail_in, tri_in, inv_ref, sum_ref,
@@ -628,13 +638,13 @@
             pltpu.VMEM((2, mates, size // (mates // 2), size), f32),
             pltpu.VMEM((2, 2 * size, size), f32),
             pltpu.SemaphoreType.DMA((2,)),
-            pltpu.SemaphoreType.DMA((11,)),
-            pltpu.SemaphoreType.DMA((11,)),
-            pltpu.SemaphoreType.DMA((2 * mates + 1,)),
-            pltpu.SemaphoreType.DMA((2 * mates + 1,)),
-            pltpu.SemaphoreType.DMA((4 * mates + 4,)),
-            pltpu.SemaphoreType.DMA((4 * mates + 4,)),
-            pltpu.SemaphoreType.REGULAR((3,)),
+            pltpu.SemaphoreType.DMA((1,)),
+            pltpu.SemaphoreType.DMA((5,)),
+            pltpu.SemaphoreType.DMA((2,)),
+            pltpu.SemaphoreType.DMA((5,)),
+            pltpu.SemaphoreType.DMA((5,)),
+            pltpu.SemaphoreType.DMA((8,)),
+            pltpu.SemaphoreType.REGULAR((4,)),
         ],
         compiler_params=pltpu.CompilerParams(
             collective_id=0, has_side_effects=True, vmem_limit_bytes=VMEM_BYTES),

time: 37.1 us -> 35.2 us (0.949)
  Pallas kernels: 36 us -> 34.1 us
    pallas_call x1, Pallas kernels: 34.9 us -> 33.1 us  [fused(): pl.pallas_call(functools.partial(kernel, row_count, scaling), out_shape=(...]
where the time goes in v2:
time: 35.2 us; the launch traced here: 34.8 us
  Pallas kernels  34.1 us (97%)
  between operations  0.64 us (2%)
    pallas_call x1, Pallas kernels, fused(): pl.pallas_call(functools.partial(kernel, row_count, scaling), out_shape=(...  33.1 us
    pallas_call x1, Pallas kernels, fused(): pl.pallas_call(functools.partial(finish_kernel, scaling), out_shape=(orth...  1.08 us

profile of v2, /device:TPU:0, one launch (start us, length us, event | category | flops | bytes accessed | tf_op | source)
XLA Modules:
  0.0 34.8 jit_solution(9284254453974045609)
XLA Ops:
  0.6 33.1 %shard_map.38 = (f32[128,1024]{1,0:T(8,128)S(1)}, f32[128,1024]{1,0:T(8,128)S(1)}, f32[128,256]{1,0:T(8,128)S(1)}, f32[128,256]{1,0:T(8,128)S(1)}, f32[2,256,128]{2,1,0:T(8,128)S(1)}) custom-call(f32[256,1024]{1,0:T(8,128)} %x_ref.1), custom_call_target="tpu_custom_call" | custom-call | tf_op jit(solution)/shard_map/pallas_call | solution.py:613
  33.7 1.1 %shard_map.39 = (f32[128,1024]{1,0:T(8,128)}, f32[128,512]{1,0:T(8,128)}, f32[128,1024]{1,0:T(8,128)}) custom-call(f32[128,1024]{1,0:T(8,128)S(1)} %get-tuple-element.8.q_in, f32[128,1024]{1,0:T(8,128)S(1)} %get-tuple-element.9.tail_in, f32[128,256]{1,0:T(8,128)S(1)} %get-tuple-element.10.tri_in, f32[128,256]{1,0:T(8,128)S(1)} %get-tuple-element.11.inv_ref, ...), custom_call_target="tpu_custom_call" | custom-call | tf_op jit(solution)/shard_map/pallas_call | solution.py:652

commit v3 on v2

--- a/solution.py
+++ b/solution.py
@@ -95,7 +95,7 @@
 
 
 def kernel(row_count, scaling, x_ref, q_ref, tail_ref, tri_ref, inv_ref, sum_ref,
-           xs, ys, part, gram, pair_in, ring_in, first, second, inverse, power, z_ref,
+           xs, ys, part, gram, pair_in, ring_in, first, second, inverse, factors, z_ref,
            xy, xy_pair, xy_ring, xy_all, load, x_send, x_recv, g_send, g_recv,
            y_send, y_recv, relay):
     r = lax.axis_index("rows")
@@ -173,14 +173,13 @@
 
     x_views = (
         [(rows, late) for rows in top]
-        + [(rows, cols(4, 2)) for rows in bottom]
-        + [(rows, cols(6, 2)) for rows in bottom]
+        + [(rows, late) for rows in bottom]
         + [(every, cols(0, 1)), (pl.ds(0, size), cols(1, 1)), (pl.ds(size, size), cols(1, 1)),
            (every, cols(2, 1)), (every, cols(3, 1))]
     )
     y_views = [(pl.ds(0, size), early), (pl.ds(size, size), early), (pl.ds(0, size), late)]
 
-    x_group = (0, 0, 1, 1, 1, 1, 2, 3, 3, 3, 4)
+    x_group = (0, 0, 1, 1, 2, 2, 2, 2, 3)
 
     def x_copy(q):
         return push(x_ref.at[x_views[q]], xs.at[x_views[q]], x_send.at[0],
@@ -192,7 +191,7 @@
     def bulk(ref, send_sem, recv_sem):
         return push(ref, ref, send_sem, recv_sem, across)
 
-    x_sizes = ((size, late), (size, late), (2 * size, cols(0, 1)), (2 * size, cols(1, 2)),
+    x_sizes = ((size, late), (size, late), (2 * size, cols(0, 3)),
                (2 * size, cols(3, 1)))
 
     def x_group_wait(g):
@@ -210,7 +209,7 @@
 
     @pl.when(c == 0)
     def _():
-        for q in range(4):
+        for q in range(5):
             x_copy(q).start()
 
     @pl.when(c == 1)
@@ -270,10 +269,12 @@
                     g_recv.at[1], at(mate(k), c))
 
     def g_cross():
-        return push(gram.at[own], gram.at[own], g_send.at[0], g_recv.at[2], across)
+        return push(gram.at[own], gram.at[own], g_send.at[0], g_recv.at[2], (side[0], other))
+
+    held = piece(h + c * (1 - 2 * lax.rem(h, 2)))
 
     def g_gather(k):
-        return push(gram.at[own], gram.at[own], g_send.at[1], g_recv.at[3], at(mate(k), c))
+        return push(gram.at[held], gram.at[held], g_send.at[1], g_recv.at[3], at(mate(k), c))
 
     def g_half(rows):
         return push(gram.at[rows], gram.at[rows], g_send.at[1], g_recv.at[4], partner)
@@ -281,11 +282,9 @@
     def amount(ref, send_sem, recv_sem):
         return push(ref, ref, send_sem, recv_sem, partner)
 
-    first_owner = mates // 4
-    owners = range(first_owner, mates - first_owner)
+    owners = range(mates)
     split = mates // 2
-    rows_chunk = size // len(owners)
-    is_owner = (h >= first_owner) & (h < mates - first_owner)
+    rows_chunk = size // mates
 
     def rows_at(offset, count):
         return pl.ds(pl.multiple_of(offset, 8), count)
@@ -294,7 +293,7 @@
     y_his = rows_at((1 - parity) * size, size)
 
     def y_piece(idx):
-        return rows_at(parity * size + (idx - first_owner) * rows_chunk, rows_chunk)
+        return rows_at(parity * size + idx * rows_chunk, rows_chunk)
 
     def y_pair(q):
         if q < 2:
@@ -324,24 +323,18 @@
 
     def y_share(j):
         view = xy_all.at[c, y_piece(h)]
-        return push(view, view, y_send.at[2], y_recv.at[share], at(j, c))
+        return push(view, view, y_send.at[1], y_recv.at[share], at(j, c))
 
     def y_lend(j):
         view = xy_all.at[c, y_piece(h)]
-        return push(view, view, y_send.at[3], y_recv.at[lend], at(j, other))
+        return push(view, view, y_send.at[1], y_recv.at[lend], at(j, other))
 
     def y_half(which, plane, rows):
         view = xy_all.at[plane, rows]
-        return push(view, view, y_send.at[4], y_recv.at[final + which], partner)
-
-    def by_role(count, step):
-        @pl.when(is_owner)
-        def _():
-            step(count - 1)
-
-        @pl.when(jnp.logical_not(is_owner))
-        def _():
-            step(count)
+        return push(view, view, y_send.at[2], y_recv.at[final + which], partner)
+
+    lends = (c == 0) | (parity == 0)
+    borrows = (c == 1) | (parity == 0)
 
     def unless_self(j, step):
         @pl.when(h != j)
@@ -351,13 +344,13 @@
     def scatter(q):
         y_pair(q).wait_recv()
         y_merge(q)
-        targets = owners if q < 2 else [j for j in owners if (j >= split) == (q == 3)]
-        if q != 0:
-            for j in targets:
+        if q in (1, 3):
+            for j in owners:
                 y_far(j).start()
         if q != 1:
-            for j in targets:
-                unless_self(j, y_near(j).start)
+            for j in owners:
+                if q == 0 or (j >= split) == (q == 3):
+                    unless_self(j, y_near(j).start)
 
     def meet(q):
         if q < 2:
@@ -403,8 +396,6 @@
             total = total + ring_in[k]
         gram[own] = total
         g_cross().start()
-        for q in range(4, 7):
-            x_copy(q).start()
 
     @pl.when(c == 1)
     def _():
@@ -414,7 +405,7 @@
         meet(2)
         pl.semaphore_wait(relay.at[2], 1)
         scatter(2)
-        g_cross().wait_recv()
+        amount(gram.at[held], g_send.at[0], g_recv.at[2]).wait_recv()
 
     for k in range(1, mates):
         g_gather(k).start()
@@ -451,39 +442,37 @@
             step()
 
     def meet_last():
+        x_copy(5).start()
         y_copy(1).wait_recv()
-        x_copy(7).start()
         meet(1)
 
     def scatter_last():
         pl.semaphore_wait(relay.at[2], 1)
         scatter(1)
-        for q in range(8, 10):
+        for q in range(6, 9):
             x_copy(q).start()
 
     def gather():
-        @pl.when(is_owner)
-        def _():
-            amount(xy_ring.at[0, pl.ds(0, mates - 1)], y_send.at[1], y_recv.at[near]).wait_recv()
-            amount(xy_ring.at[1], y_send.at[0], y_recv.at[far]).wait_recv()
-            total = xy[c, y_piece(h)]
-            for k in range(1, mates):
-                total = total + xy_ring[0, mate(k)]
-            for j in range(mates):
-                total = total + xy_ring[1, j]
-            xy_all[c, y_piece(h)] = total
-            for j in range(mates):
-                unless_self(j, y_share(j).start)
+        amount(xy_ring.at[0, pl.ds(0, mates - 1)], y_send.at[1], y_recv.at[near]).wait_recv()
+        amount(xy_ring.at[1], y_send.at[0], y_recv.at[far]).wait_recv()
+        total = xy[c, y_piece(h)]
+        for k in range(1, mates):
+            total = total + xy_ring[0, mate(k)]
+        for j in range(mates):
+            total = total + xy_ring[1, j]
+        xy_all[c, y_piece(h)] = total
+        for j in range(mates):
+            unless_self(j, y_share(j).start)
+
+        @pl.when(lends)
+        def _():
             for j in range(mates):
                 y_lend(j).start()
-
-        @pl.when(c == 0)
-        def _():
-            x_copy(10).start()
 
     eliminate(first, {
         0: lambda: on_plane(0, meet_last),
         2: lambda: on_plane(0, scatter_last),
+        7: lambda: on_plane(1, gather),
     })
 
     upper = first[:, size:2 * size]
@@ -492,20 +481,20 @@
     second[:, size:2 * size] = -cross[:, size:]
     second[:, 2 * size:] = eye
     eliminate(second, {
-        1: lambda: on_plane(1, gather),
         3: lambda: on_plane(0, gather),
     })
 
     inverse[:size, :size] = first[:, 2 * size:]
     inverse[:size, size:] = jnp.zeros((size, size), jnp.float32)
     inverse[size:] = second[:, size:]
-    power[...] = contract(inverse[...], inverse[...], ((0,), (0,)))
     own_rows = pl.ds(pl.multiple_of(c * size, size), size)
+    factors[:size] = inverse[own_rows]
+    factors[size:] = contract(inverse[...], inverse[...], ((0,), (0,)))
 
     def products(lo, count):
         span = pl.ds(lo * eighth, count * eighth)
-        q_ref[:, span] = product(inverse[own_rows], xs[:, span]) * scaling
-        z_ref[:, span] = product(power[...], xs[:, span])
+        q_ref[:, span] = product(factors[:size], xs[:, span]) * scaling
+        z_ref[:, span] = product(factors[size:], xs[:, span])
 
     keep = (lax.broadcasted_iota(jnp.int32, (size, size), 0)
             <= lax.broadcasted_iota(jnp.int32, (size, size), 1))
@@ -525,56 +514,76 @@
     def _():
         tri_ref[:, :size] = jnp.zeros((size, size), jnp.float32)
         tri_ref[:, size:2 * size] = jnp.where(keep, second[:, :size], 0.0) / scaling
-        x_group_wait(2)
-
-    inv_ref[...] = inverse[own_rows]
-    products(4, 4)
-    products(0, 1)
-
-    @pl.when(c == 1)
-    def _():
-        x_group_wait(3)
-
-    products(1, 2)
-
-    @pl.when(c == 0)
-    def _():
-        products(3, 1)
-        amount(part, g_send.at[0], g_recv.at[0]).wait_send()
-
-    amount(gram.at[pl.ds(0, (mates - 1) * chunk + half)], g_send.at[1], g_recv.at[0]).wait_send()
-    amount(part, y_send.at[0], y_recv.at[0]).wait_send()
-
+
+    inv_ref[...] = factors[:size]
     def rows_of(count):
         return xy_all.at[0, pl.ds(0, count * rows_chunk)]
 
-    by_role(len(owners), lambda n: amount(
-        rows_of(n), y_send.at[1], y_recv.at[0]).wait_send())
-    by_role(len(owners), lambda n: amount(
-        rows_of(n), y_send.at[1], y_recv.at[share]).wait_recv())
-    y_half(0, c, y_mine).start()
-    amount(rows_of(len(owners)), y_send.at[1], y_recv.at[lend]).wait_recv()
-    y_half(1, other, y_mine).start()
-    y_half(0, c, y_his).wait_recv()
-    trail(4, 4)
-    trail(0, 3)
-    sum_ref[c] = xy_all[c]
-
-    @pl.when(is_owner)
-    def _():
-        amount(rows_of(mates - 1), y_send.at[2], y_recv.at[0]).wait_send()
-        amount(rows_of(mates), y_send.at[3], y_recv.at[0]).wait_send()
+    def take_own():
+        amount(rows_of(mates - 1), y_send.at[1], y_recv.at[share]).wait_recv()
+        y_half(0, c, y_mine).start()
+
+    def take_other():
+        amount(rows_of(mates), y_send.at[1], y_recv.at[lend]).wait_recv()
+        y_half(1, other, y_mine).start()
+
+    def sent():
+        amount(gram.at[pl.ds(0, (mates - 1) * chunk + half)], g_send.at[1],
+               g_recv.at[0]).wait_send()
+        amount(part, y_send.at[0], y_recv.at[0]).wait_send()
+        amount(xy_pair.at[0], y_send.at[2], y_recv.at[0]).wait_send()
+
+        @pl.when(lends)
+        def _():
+            amount(part.at[pl.ds(0, (3 * mates - 2) * rows_chunk)], y_send.at[1],
+                   y_recv.at[0]).wait_send()
+
+        @pl.when(jnp.logical_not(lends))
+        def _():
+            amount(part.at[pl.ds(0, (2 * mates - 2) * rows_chunk)], y_send.at[1],
+                   y_recv.at[0]).wait_send()
+
+        sum_ref[c] = xy_all[c]
+
+    products(4, 4)
+
+    @pl.when(c == 0)
+    def _():
+        products(0, 4)
+        amount(part, g_send.at[0], g_recv.at[0]).wait_send()
+        take_own()
+        y_half(0, c, y_his).wait_recv()
+        sum_ref[1, size:] = jnp.zeros((size, size), jnp.float32)
+        trail(0, 8)
+        bulk_sent()
+        sent()
+
+        @pl.when(borrows)
+        def _():
+            take_other()
+            sum_ref[1, :size] = xy_all[1, :size]
+            y_half(1, other, y_mine).wait_send()
+
+        @pl.when(jnp.logical_not(borrows))
+        def _():
+            y_half(1, other, y_his).wait_recv()
+            sum_ref[1, :size] = xy_all[1, :size]
 
     @pl.when(c == 1)
     def _():
-        x_group_wait(4)
+        take_own()
+        x_group_wait(2)
+        products(0, 3)
+        x_group_wait(3)
         products(3, 1)
-
-    bulk_sent()
-    trail(3, 1)
-    y_half(1, other, y_his).wait_recv()
-    sum_ref[other] = xy_all[other]
-    amount(xy_pair, y_send.at[4], y_recv.at[0]).wait_send()
+        take_other()
+        bulk_sent()
+        y_half(0, c, y_his).wait_recv()
+        trail(0, 8)
+        sent()
+        y_half(1, other, y_his).wait_recv()
+        sum_ref[0] = xy_all[0]
+        y_half(1, other, y_mine).wait_send()
 
 
 def finish_kernel(scaling, q_in, tail_in, tri_in, inv_ref, sum_ref,
@@ -631,18 +640,18 @@
             pltpu.VMEM((size, 3 * size), f32),
             pltpu.VMEM((size, 3 * size), f32),
             pltpu.VMEM((2 * size, 2 * size), f32),
-            pltpu.VMEM((2 * size, 2 * size), f32),
+            pltpu.VMEM((3 * size, 2 * size), f32),
             pltpu.VMEM((2 * size, width), f32),
             pltpu.VMEM((2, 2 * size, size), f32),
             pltpu.VMEM((2, size, size), f32),
-            pltpu.VMEM((2, mates, size // (mates // 2), size), f32),
+            pltpu.VMEM((2, mates, size // mates, size), f32),
             pltpu.VMEM((2, 2 * size, size), f32),
             pltpu.SemaphoreType.DMA((2,)),
             pltpu.SemaphoreType.DMA((1,)),
-            pltpu.SemaphoreType.DMA((5,)),
+            pltpu.SemaphoreType.DMA((4,)),
             pltpu.SemaphoreType.DMA((2,)),
             pltpu.SemaphoreType.DMA((5,)),
-            pltpu.SemaphoreType.DMA((5,)),
+            pltpu.SemaphoreType.DMA((3,)),
             pltpu.SemaphoreType.DMA((8,)),
             pltpu.SemaphoreType.REGULAR((4,)),
         ],

time: 35.2 us -> 34.3 us (0.974)
  Pallas kernels: 34.1 us -> 32.8 us
    pallas_call x1, Pallas kernels: 33.1 us -> 31.7 us  [fused(): pl.pallas_call(functools.partial(kernel, row_count, scaling), out_shape=(...]
where the time goes in v3:
time: 34.3 us; the launch traced here: 33.6 us
  Pallas kernels  32.8 us (96%)
  between operations  0.8 us (2%)
    pallas_call x1, Pallas kernels, fused(): pl.pallas_call(functools.partial(kernel, row_count, scaling), out_shape=(...  31.7 us
    pallas_call x1, Pallas kernels, fused(): pl.pallas_call(functools.partial(finish_kernel, scaling), out_shape=(orth...  1.08 us

profile of v3, /device:TPU:0, one launch (start us, length us, event | category | flops | bytes accessed | tf_op | source)
XLA Modules:
  0.0 33.6 jit_solution(7718960591148760881)
XLA Ops:
  0.6 31.7 %shard_map.38 = (f32[128,1024]{1,0:T(8,128)S(1)}, f32[128,1024]{1,0:T(8,128)S(1)}, f32[128,256]{1,0:T(8,128)S(1)}, f32[128,256]{1,0:T(8,128)S(1)}, f32[2,256,128]{2,1,0:T(8,128)S(1)}) custom-call(f32[256,1024]{1,0:T(8,128)} %x_ref.1), custom_call_target="tpu_custom_call" | custom-call | tf_op jit(solution)/shard_map/pallas_call | solution.py:622
  32.4 1.1 %shard_map.39 = (f32[128,1024]{1,0:T(8,128)}, f32[128,512]{1,0:T(8,128)}, f32[128,1024]{1,0:T(8,128)}) custom-call(f32[128,1024]{1,0:T(8,128)S(1)} %get-tuple-element.8.q_in, f32[128,1024]{1,0:T(8,128)S(1)} %get-tuple-element.9.tail_in, f32[128,256]{1,0:T(8,128)S(1)} %get-tuple-element.10.tri_in, f32[128,256]{1,0:T(8,128)S(1)} %get-tuple-element.11.inv_ref, ...), custom_call_target="tpu_custom_call" | custom-call | tf_op jit(solution)/shard_map/pallas_call | solution.py:661

commit v4 on v3

--- a/solution.py
+++ b/solution.py
@@ -46,46 +46,79 @@
     return jnp.dot(lhs.T[after:], rhs, preferred_element_type=jnp.float32)
 
 
-def root_inverse(value):
-    guess = lax.rsqrt(value)
-    return guess * (1.5 - (0.5 * value) * guess * guess)
+def spread(value, i):
+    return jnp.broadcast_to(value[i:i + 1], value.shape)
 
 
 def eliminate(ref, hooks):
     size = ref.shape[0]
     lanes = size
     parts = ref.shape[1] // lanes
-    below = lax.broadcasted_iota(jnp.int32, (STRIP, lanes), 0)
+    tall = STRIP // 2
+    below = lax.broadcasted_iota(jnp.int32, (tall, lanes), 0)
+
+    def column(value, j):
+        return jnp.broadcast_to(value[:, j:j + 1], (tall, lanes))
+
+    def diagonal(cols):
+        value = cols[0]
+        for j in range(1, tall):
+            value = jnp.where(below == j, cols[j], value)
+        return value
+
     for s in range(size // STRIP):
         at = s * STRIP
-        rows = [ref[at:at + STRIP, q * lanes:(q + 1) * lanes] for q in range(parts)]
-        cols = [
-            jnp.broadcast_to(rows[0][:, at + j:at + j + 1], (STRIP, lanes))
-            for j in range(STRIP)
-        ]
-        scales = [lax.rsqrt(cols[i][i:i + 1]) for i in range(0, STRIP, 2)]
+        spans = [slice(q * lanes, (q + 1) * lanes) for q in range(parts)]
+        upper = [ref[at:at + tall, span] for span in spans]
+        lower = [ref[at + tall:at + STRIP, span] for span in spans]
+        tops = [column(upper[0], at + j) for j in range(tall)]
+        lows = [column(lower[0], at + j) for j in range(STRIP)]
+        scale_top = lax.rsqrt(diagonal(tops))
+        scale_low = lax.rsqrt(diagonal(lows[tall:]))
+        upper = [value * scale_top for value in upper]
+        lower = [value * scale_low for value in lower]
+        for j in range(STRIP):
+            own_scale = spread(scale_top if j < tall else scale_low, j % tall)
+            lows[j] = lows[j] * scale_low * own_scale
+            if j < tall:
+                tops[j] = tops[j] * scale_top * own_scale
         for i in range(0, STRIP, 2):
-            scale = scales[i // 2]
-            corner = cols[i][i:i + 1]
-            edge = cols[i][i + 1:i + 2]
-            unit = corner * scale * scale
-            minor = unit * cols[i + 1][i + 1:i + 2] - edge * scale * scale * edge
-            inv = root_inverse(corner)
-            inv_next = root_inverse(minor) * (unit * root_inverse(unit))
-            col = cols[i] * inv
-            col_next = (cols[i + 1] - col * col[i + 1:i + 2]) * inv_next
-            coef = jnp.where(below > i, col, 0.0)
-            coef_next = jnp.where(below > i + 1, col_next, 0.0)
+            high = i < tall
+            r = i % tall
+            cur = tops if high else lows
+            rows = upper if high else lower
+            corner = spread(cur[i], r)
+            edge = spread(cur[i], r + 1)
+            minor = corner * spread(cur[i + 1], r + 1) - edge * edge
+            inv = lax.rsqrt(corner)
+            inv_next = lax.rsqrt(minor) * (corner * inv)
+            slope = edge * inv
+            col = cur[i] * inv
+            col_next = (cur[i + 1] - col * slope) * inv_next
+            coef = jnp.where(below > r, col, 0.0)
+            coef_next = jnp.where(below > r + 1, col_next, 0.0)
+            if high:
+                tail = lows[i] * inv
+                tail_next = (lows[i + 1] - tail * slope) * inv_next
             for j in range(i + 2, STRIP):
-                cols[j] = cols[j] - coef * col[j:j + 1] - coef_next * col_next[j:j + 1]
+                same = high == (j < tall)
+                one = spread(col if same else tail, j % tall)
+                two = spread(col_next if same else tail_next, j % tall)
+                if same:
+                    cur[j] = (cur[j] - coef * one) - coef_next * two
+                if high:
+                    lows[j] = (lows[j] - tail * one) - tail_next * two
             for q in range(parts):
-                row = rows[q][i:i + 1] * inv
+                row = spread(rows[q], r) * inv
                 rest = rows[q] - coef * row
-                row_next = rest[i + 1:i + 2] * inv_next
-                rest = jnp.where(below == i + 1, row_next, rest - coef_next * row_next)
-                rows[q] = jnp.where(below == i, row, rest)
+                row_next = spread(rest, r + 1) * inv_next
+                rest = jnp.where(below == r + 1, row_next, rest - coef_next * row_next)
+                rows[q] = jnp.where(below == r, row, rest)
+                if high:
+                    lower[q] = (lower[q] - tail * row) - tail_next * row_next
+        rows = [jnp.concatenate([upper[q], lower[q]], axis=0) for q in range(parts)]
         for q in range(parts):
-            ref[at:at + STRIP, q * lanes:(q + 1) * lanes] = rows[q]
+            ref[at:at + STRIP, spans[q]] = rows[q]
         after = at + STRIP
         if after < size:
             update = strip_update(rows[0], jnp.concatenate(rows, axis=1), after)
@@ -325,16 +358,14 @@
         view = xy_all.at[c, y_piece(h)]
         return push(view, view, y_send.at[1], y_recv.at[share], at(j, c))
 
-    def y_lend(j):
+    def y_lend(j, side_core=0):
         view = xy_all.at[c, y_piece(h)]
-        return push(view, view, y_send.at[1], y_recv.at[lend], at(j, other))
+        row = j * 2 + (1 - parity if side_core else parity)
+        return push(view, view, y_send.at[1], y_recv.at[lend], (row, other))
 
     def y_half(which, plane, rows):
         view = xy_all.at[plane, rows]
         return push(view, view, y_send.at[2], y_recv.at[final + which], partner)
-
-    lends = (c == 0) | (parity == 0)
-    borrows = (c == 1) | (parity == 0)
 
     def unless_self(j, step):
         @pl.when(h != j)
@@ -442,14 +473,15 @@
             step()
 
     def meet_last():
-        x_copy(5).start()
+        for q in range(5, 7):
+            x_copy(q).start()
         y_copy(1).wait_recv()
         meet(1)
 
     def scatter_last():
         pl.semaphore_wait(relay.at[2], 1)
         scatter(1)
-        for q in range(6, 9):
+        for q in range(7, 9):
             x_copy(q).start()
 
     def gather():
@@ -464,10 +496,16 @@
         for j in range(mates):
             unless_self(j, y_share(j).start)
 
-        @pl.when(lends)
+        @pl.when(c == 0)
         def _():
             for j in range(mates):
                 y_lend(j).start()
+
+        @pl.when((c == 1) & (parity == 0))
+        def _():
+            for j in range(mates):
+                for core in range(2):
+                    y_lend(j, core).start()
 
     eliminate(first, {
         0: lambda: on_plane(0, meet_last),
@@ -525,24 +563,16 @@
 
     def take_other():
         amount(rows_of(mates), y_send.at[1], y_recv.at[lend]).wait_recv()
-        y_half(1, other, y_mine).start()
-
-    def sent():
+
+    def sent(pieces_sent):
+        rows = pieces_sent * rows_chunk // 2
+        amount(xy.at[:, pl.ds(0, rows)], y_send.at[1], y_recv.at[0]).wait_send()
+
+    def all_sent():
         amount(gram.at[pl.ds(0, (mates - 1) * chunk + half)], g_send.at[1],
                g_recv.at[0]).wait_send()
         amount(part, y_send.at[0], y_recv.at[0]).wait_send()
-        amount(xy_pair.at[0], y_send.at[2], y_recv.at[0]).wait_send()
-
-        @pl.when(lends)
-        def _():
-            amount(part.at[pl.ds(0, (3 * mates - 2) * rows_chunk)], y_send.at[1],
-                   y_recv.at[0]).wait_send()
-
-        @pl.when(jnp.logical_not(lends))
-        def _():
-            amount(part.at[pl.ds(0, (2 * mates - 2) * rows_chunk)], y_send.at[1],
-                   y_recv.at[0]).wait_send()
-
+        bulk_sent()
         sum_ref[c] = xy_all[c]
 
     products(4, 4)
@@ -555,35 +585,35 @@
         y_half(0, c, y_his).wait_recv()
         sum_ref[1, size:] = jnp.zeros((size, size), jnp.float32)
         trail(0, 8)
-        bulk_sent()
-        sent()
-
-        @pl.when(borrows)
-        def _():
-            take_other()
-            sum_ref[1, :size] = xy_all[1, :size]
-            y_half(1, other, y_mine).wait_send()
-
-        @pl.when(jnp.logical_not(borrows))
-        def _():
-            y_half(1, other, y_his).wait_recv()
-            sum_ref[1, :size] = xy_all[1, :size]
+        all_sent()
+        amount(xy_pair.at[0], y_send.at[2], y_recv.at[0]).wait_send()
+        sent(3 * mates - 2)
+        take_other()
+        sum_ref[1, :size] = xy_all[1, :size]
 
     @pl.when(c == 1)
     def _():
         take_own()
-        x_group_wait(2)
-        products(0, 3)
-        x_group_wait(3)
-        products(3, 1)
+        for g in range(2, 4):
+            x_group_wait(g)
+        products(0, 4)
         take_other()
-        bulk_sent()
+        y_half(1, other, y_mine).start()
         y_half(0, c, y_his).wait_recv()
         trail(0, 8)
-        sent()
+        all_sent()
+
+        @pl.when(parity == 0)
+        def _():
+            sent(4 * mates - 2)
+
+        @pl.when(parity == 1)
+        def _():
+            sent(2 * mates - 2)
+
         y_half(1, other, y_his).wait_recv()
         sum_ref[0] = xy_all[0]
-        y_half(1, other, y_mine).wait_send()
+        amount(xy_pair, y_send.at[2], y_recv.at[0]).wait_send()
 
 
 def finish_kernel(scaling, q_in, tail_in, tri_in, inv_ref, sum_ref,

time: 34.3 us -> 33.1 us (0.965)
  Pallas kernels: 32.8 us -> 31.9 us
    pallas_call x1, Pallas kernels: 31.7 us -> 30.9 us  [fused(): pl.pallas_call(functools.partial(kernel, row_count, scaling), out_shape=(...]
where the time goes in v4:
time: 33.1 us; the launch traced here: 32.6 us
  Pallas kernels  31.9 us (96%)
  between operations  0.64 us (2%)
    pallas_call x1, Pallas kernels, fused(): pl.pallas_call(functools.partial(kernel, row_count, scaling), out_shape=(...  30.9 us
    pallas_call x1, Pallas kernels, fused(): pl.pallas_call(functools.partial(finish_kernel, scaling), out_shape=(orth...  1.08 us

profile of v4, /device:TPU:0, one launch (start us, length us, event | category | flops | bytes accessed | tf_op | source)
XLA Modules:
  0.0 32.6 jit_solution(6484879513694897279)
XLA Ops:
  0.6 30.9 %shard_map.38 = (f32[128,1024]{1,0:T(8,128)S(1)}, f32[128,1024]{1,0:T(8,128)S(1)}, f32[128,256]{1,0:T(8,128)S(1)}, f32[128,256]{1,0:T(8,128)S(1)}, f32[2,256,128]{2,1,0:T(8,128)S(1)}) custom-call(f32[256,1024]{1,0:T(8,128)} %x_ref.1), custom_call_target="tpu_custom_call" | custom-call | tf_op jit(solution)/shard_map/pallas_call | solution.py:652
  31.5 1.1 %shard_map.39 = (f32[128,1024]{1,0:T(8,128)}, f32[128,512]{1,0:T(8,128)}, f32[128,1024]{1,0:T(8,128)}) custom-call(f32[128,1024]{1,0:T(8,128)S(1)} %get-tuple-element.8.q_in, f32[128,1024]{1,0:T(8,128)S(1)} %get-tuple-element.9.tail_in, f32[128,256]{1,0:T(8,128)S(1)} %get-tuple-element.10.tri_in, f32[128,256]{1,0:T(8,128)S(1)} %get-tuple-element.11.inv_ref, ...), custom_call_target="tpu_custom_call" | custom-call | tf_op jit(solution)/shard_map/pallas_call | solution.py:691

commit v5 on v4

--- a/solution.py
+++ b/solution.py
@@ -458,6 +458,8 @@
     @pl.when(c == 0)
     def _():
         scatter(0)
+        for q in range(5, 7):
+            x_copy(q).start()
 
     g_half(his).wait_recv()
 
@@ -473,8 +475,6 @@
             step()
 
     def meet_last():
-        for q in range(5, 7):
-            x_copy(q).start()
         y_copy(1).wait_recv()
         meet(1)
 

time: 33.1 us -> 33.6 us (1.015); the launches traced: 32.6 us -> 33.4 us
  Pallas kernels: 31.9 us -> 32.8 us
    pallas_call x1, Pallas kernels: 30.9 us -> 31.7 us  [fused(): pl.pallas_call(functools.partial(kernel, row_count, scaling), out_shape=(...]
where the time goes in v5:
time: 33.6 us; the launch traced here: 33.4 us
  Pallas kernels  32.8 us (98%)
  between operations  0.64 us (2%)
    pallas_call x1, Pallas kernels, fused(): pl.pallas_call(functools.partial(kernel, row_count, scaling), out_shape=(...  31.7 us
    pallas_call x1, Pallas kernels, fused(): pl.pallas_call(functools.partial(finish_kernel, scaling), out_shape=(orth...  1.08 us

profile of v5, /device:TPU:0, one launch (start us, length us, event | category | flops | bytes accessed | tf_op | source)
XLA Modules:
  0.0 33.4 jit_solution(13543069367529192010)
XLA Ops:
  0.6 31.7 %shard_map.38 = (f32[128,1024]{1,0:T(8,128)S(1)}, f32[128,1024]{1,0:T(8,128)S(1)}, f32[128,256]{1,0:T(8,128)S(1)}, f32[128,256]{1,0:T(8,128)S(1)}, f32[2,256,128]{2,1,0:T(8,128)S(1)}) custom-call(f32[256,1024]{1,0:T(8,128)} %x_ref.1), custom_call_target="tpu_custom_call" | custom-call | tf_op jit(solution)/shard_map/pallas_call | solution.py:652
  32.4 1.1 %shard_map.39 = (f32[128,1024]{1,0:T(8,128)}, f32[128,512]{1,0:T(8,128)}, f32[128,1024]{1,0:T(8,128)}) custom-call(f32[128,1024]{1,0:T(8,128)S(1)} %get-tuple-element.8.q_in, f32[128,1024]{1,0:T(8,128)S(1)} %get-tuple-element.9.tail_in, f32[128,256]{1,0:T(8,128)S(1)} %get-tuple-element.10.tri_in, f32[128,256]{1,0:T(8,128)S(1)} %get-tuple-element.11.inv_ref, ...), custom_call_target="tpu_custom_call" | custom-call | tf_op jit(solution)/shard_map/pallas_call | solution.py:691

commit v6 on v5

--- a/solution.py
+++ b/solution.py
@@ -458,8 +458,6 @@
     @pl.when(c == 0)
     def _():
         scatter(0)
-        for q in range(5, 7):
-            x_copy(q).start()
 
     g_half(his).wait_recv()
 
@@ -475,13 +473,14 @@
             step()
 
     def meet_last():
+        x_copy(5).start()
         y_copy(1).wait_recv()
         meet(1)
 
     def scatter_last():
         pl.semaphore_wait(relay.at[2], 1)
         scatter(1)
-        for q in range(7, 9):
+        for q in range(6, 9):
             x_copy(q).start()
 
     def gather():

time: 33.6 us -> 34.2 us (1.018)
  the two profiles are of different devices: /device:TPU:0 before, /device:TPU:5 now
where the time goes in v6:
time: 34.2 us; the launch traced here: 34.1 us
  Pallas kernels  33.4 us (98%)
  between operations  0.64 us (2%)
    pallas_call x1, Pallas kernels, fused(): pl.pallas_call(functools.partial(kernel, row_count, scaling), out_shape=(...  32.4 us
    pallas_call x1, Pallas kernels, fused(): pl.pallas_call(functools.partial(finish_kernel, scaling), out_shape=(orth...  1.08 us

profile of v6, /device:TPU:5, one launch (start us, length us, event | category | flops | bytes accessed | tf_op | source)
XLA Modules:
  0.0 34.1 jit_solution(13113990469816716873)
XLA Ops:
  0.6 32.4 %shard_map.38 = (f32[128,1024]{1,0:T(8,128)S(1)}, f32[128,1024]{1,0:T(8,128)S(1)}, f32[128,256]{1,0:T(8,128)S(1)}, f32[128,256]{1,0:T(8,128)S(1)}, f32[2,256,128]{2,1,0:T(8,128)S(1)}) custom-call(f32[256,1024]{1,0:T(8,128)} %x_ref.1), custom_call_target="tpu_custom_call" | custom-call | tf_op jit(solution)/shard_map/pallas_call | solution.py:651
  33.0 1.1 %shard_map.39 = (f32[128,1024]{1,0:T(8,128)}, f32[128,512]{1,0:T(8,128)}, f32[128,1024]{1,0:T(8,128)}) custom-call(f32[128,1024]{1,0:T(8,128)S(1)} %get-tuple-element.8.q_in, f32[128,1024]{1,0:T(8,128)S(1)} %get-tuple-element.9.tail_in, f32[128,256]{1,0:T(8,128)S(1)} %get-tuple-element.10.tri_in, f32[128,256]{1,0:T(8,128)S(1)} %get-tuple-element.11.inv_ref, ...), custom_call_target="tpu_custom_call" | custom-call | tf_op jit(solution)/shard_map/pallas_call | solution.py:690

commit v7 on v4

--- a/solution.py
+++ b/solution.py
@@ -212,7 +212,7 @@
     )
     y_views = [(pl.ds(0, size), early), (pl.ds(size, size), early), (pl.ds(0, size), late)]
 
-    x_group = (0, 0, 1, 1, 2, 2, 2, 2, 3)
+    x_group = (0, 0, 1, 1, 2, 2, 2, 3, 3)
 
     def x_copy(q):
         return push(x_ref.at[x_views[q]], xs.at[x_views[q]], x_send.at[0],
@@ -224,8 +224,8 @@
     def bulk(ref, send_sem, recv_sem):
         return push(ref, ref, send_sem, recv_sem, across)
 
-    x_sizes = ((size, late), (size, late), (2 * size, cols(0, 3)),
-               (2 * size, cols(3, 1)))
+    x_sizes = ((size, late), (size, late), (2 * size, cols(0, 2)),
+               (2 * size, cols(2, 2)))
 
     def x_group_wait(g):
         rows, span = x_sizes[g]
@@ -568,12 +568,10 @@
         rows = pieces_sent * rows_chunk // 2
         amount(xy.at[:, pl.ds(0, rows)], y_send.at[1], y_recv.at[0]).wait_send()
 
-    def all_sent():
+    def early_sent():
         amount(gram.at[pl.ds(0, (mates - 1) * chunk + half)], g_send.at[1],
                g_recv.at[0]).wait_send()
         amount(part, y_send.at[0], y_recv.at[0]).wait_send()
-        bulk_sent()
-        sum_ref[c] = xy_all[c]
 
     products(4, 4)
 
@@ -581,36 +579,40 @@
     def _():
         products(0, 4)
         amount(part, g_send.at[0], g_recv.at[0]).wait_send()
+        early_sent()
+        sum_ref[1, size:] = jnp.zeros((size, size), jnp.float32)
         take_own()
         y_half(0, c, y_his).wait_recv()
-        sum_ref[1, size:] = jnp.zeros((size, size), jnp.float32)
         trail(0, 8)
-        all_sent()
+        bulk_sent()
+        sent(3 * mates - 2)
+        sum_ref[c] = xy_all[c]
         amount(xy_pair.at[0], y_send.at[2], y_recv.at[0]).wait_send()
-        sent(3 * mates - 2)
         take_other()
         sum_ref[1, :size] = xy_all[1, :size]
 
     @pl.when(c == 1)
     def _():
         take_own()
-        for g in range(2, 4):
-            x_group_wait(g)
+        early_sent()
+        bulk_sent()
+
+        @pl.when(parity == 0)
+        def _():
+            sent(4 * mates - 2)
+
+        @pl.when(parity == 1)
+        def _():
+            sent(2 * mates - 2)
+
+        x_group_wait(2)
+        x_group_wait(3)
         products(0, 4)
         take_other()
         y_half(1, other, y_mine).start()
         y_half(0, c, y_his).wait_recv()
         trail(0, 8)
-        all_sent()
-
-        @pl.when(parity == 0)
-        def _():
-            sent(4 * mates - 2)
-
-        @pl.when(parity == 1)
-        def _():
-            sent(2 * mates - 2)
-
+        sum_ref[c] = xy_all[c]
         y_half(1, other, y_his).wait_recv()
         sum_ref[0] = xy_all[0]
         amount(xy_pair, y_send.at[2], y_recv.at[0]).wait_send()

time: 33.1 us -> 33.1 us (level)
  no operation moved by 1% of the time
where the time goes in v7:
time: 33.1 us; the launch traced here: 32.6 us
  Pallas kernels  31.9 us (96%)
  between operations  0.64 us (2%)
    pallas_call x1, Pallas kernels, fused(): pl.pallas_call(functools.partial(kernel, row_count, scaling), out_shape=(...  30.9 us
    pallas_call x1, Pallas kernels, fused(): pl.pallas_call(functools.partial(finish_kernel, scaling), out_shape=(orth...  1.08 us

profile of v7, /device:TPU:0, one launch (start us, length us, event | category | flops | bytes accessed | tf_op | source)
XLA Modules:
  0.0 32.6 jit_solution(10090672801665518811)
XLA Ops:
  0.6 30.9 %shard_map.38 = (f32[128,1024]{1,0:T(8,128)S(1)}, f32[128,1024]{1,0:T(8,128)S(1)}, f32[128,256]{1,0:T(8,128)S(1)}, f32[128,256]{1,0:T(8,128)S(1)}, f32[2,256,128]{2,1,0:T(8,128)S(1)}) custom-call(f32[256,1024]{1,0:T(8,128)} %x_ref.1), custom_call_target="tpu_custom_call" | custom-call | tf_op jit(solution)/shard_map/pallas_call | solution.py:654
  31.5 1.1 %shard_map.39 = (f32[128,1024]{1,0:T(8,128)}, f32[128,512]{1,0:T(8,128)}, f32[128,1024]{1,0:T(8,128)}) custom-call(f32[128,1024]{1,0:T(8,128)S(1)} %get-tuple-element.8.q_in, f32[128,1024]{1,0:T(8,128)S(1)} %get-tuple-element.9.tail_in, f32[128,256]{1,0:T(8,128)S(1)} %get-tuple-element.10.tri_in, f32[128,256]{1,0:T(8,128)S(1)} %get-tuple-element.11.inv_ref, ...), custom_call_target="tpu_custom_call" | custom-call | tf_op jit(solution)/shard_map/pallas_call | solution.py:693
